TPU v7x, 128 devices: a whole 4x4x4 slice. The times are simulated.
128 devices in a mesh: dp: 16 (over y, x), tensor: 8 (over z, core).
Axes of the slice: x: 4, y: 4, z: 4, core: 2. Of those that a mesh axis runs over, the one named last changes fastest.
Arguments:
- teacher_in: bfloat16 [4096, 2048], P('dp'), may hold values from -13 to 13
- teacher_gain: float32 [2, 2048], replicated, may hold values from 0.25 to 1.75
- t_gate: bfloat16 [2, 2048, 5472], P(None, 'dp', 'tensor'), may hold values from -0.125 to 0.125
- t_up: bfloat16 [2, 2048, 5472], P(None, 'dp', 'tensor'), may hold values from -0.125 to 0.125
- t_down: bfloat16 [2, 5472, 2048], P(None, 'tensor', 'dp'), may hold values from -0.078125 to 0.078125
- student_in: bfloat16 [4096, 1024], P('dp'), may hold values from -13 to 13
- student_gain: float32 [2, 1024], replicated, may hold values from 0.3 to 3.5
- s_gate: bfloat16 [2, 1024, 4096], P(None, None, 'tensor'), may hold values from -0.1875 to 0.1875
- s_up: bfloat16 [2, 1024, 4096], P(None, None, 'tensor'), may hold values from -0.1875 to 0.1875
- s_down: bfloat16 [2, 4096, 1024], P(None, 'tensor'), may hold values from -0.09375 to 0.09375
- proj: bfloat16 [1024, 2048], P(None, 'tensor'), may hold values from -1 to 1
- layer_map: int32 [2], replicated, may hold values from 0 to 1, each once
Outputs:
- teacher_states: bfloat16 [2, 4096, 2048], P(None, ('dp', 'tensor'))
- grad_gate: float32 [2, 1024, 4096], P(None, 'dp', 'tensor')
- grad_up: float32 [2, 1024, 4096], P(None, 'dp', 'tensor')
- grad_down: float32 [2, 4096, 1024], P(None, 'tensor', 'dp')
- grad_proj: float32 [1024, 2048], P('dp', 'tensor')
- mean_error: float32 [2], replicated
- grad_rms: float32 [4], replicated
Inputs may be any that keep to these rules, and one draw needn't show every extreme that they name: `layer_map`: each teacher sublayer is matched to exactly one student sublayer.
All inputs are finite; a program needn't handle non-finite values.
Results may differ from a plain program's by a relative error of at most 0.02.
Values may be sent and summed in bfloat16 or wider, within the bound.
A program may use at most 128 MiB of HBM per device.

v0:
```python
import functools

import jax
import jax.numpy as jnp
from jax import lax
from jax.sharding import Mesh
from jax.sharding import PartitionSpec as P

DT = 2048
DS = 1024
FS = 4096
T_LAYERS = 2
S_LAYERS = 2
SEQ = 512
TENSOR = ("tensor_0", "tensor_1")
DP = ("dp_0", "dp_1")
DP_TENSOR = ("dp_0", "dp_1", "tensor_0", "tensor_1")


EPSILON = 1e-05


def sent_together(arrays, axis, dim, along):
    both = jnp.concatenate(arrays, axis=along)
    whole, at, gathered = (lax.all_gather(both, axis, axis=dim, tiled=True), 0, [])
    for a in arrays:
        gathered.append(lax.slice_in_dim(whole, at, at + a.shape[along], axis=along))
        at += a.shape[along]
    return tuple(gathered)


def gather_axes(shard, axes, dim):
    for axis in reversed(axes):
        shard = lax.all_gather(shard, axis, axis=dim, tiled=True)
    return shard


def in_blocks(shard, dim, count):
    before, after = (shard.shape[:dim], shard.shape[dim + 1 :])
    return jnp.moveaxis(shard.reshape(*before, count, -1, *after), dim, 0)


def sum_at_owner(shard, axis, dim):
    count = lax.axis_size(axis)
    blocks = lax.all_to_all(in_blocks(shard, dim, count), axis, 0, 0, tiled=True)
    return jnp.sum(blocks.astype(jnp.float32), axis=0)


def joined_along(blocks, dim):
    blocks = jnp.moveaxis(blocks, 0, dim)
    dims = blocks.shape
    return blocks.reshape(*dims[:dim], dims[dim] * dims[dim + 1], *dims[dim + 2 :])


def sent_to_all(shard, axis):
    copies = jnp.broadcast_to(shard, (lax.axis_size(axis), *shard.shape))
    return lax.all_to_all(copies, axis, split_axis=0, concat_axis=0, tiled=True)


def gathered_copies(shard, axis, dim):
    return joined_along(sent_to_all(shard, axis), dim)


def total_of_pieces(shard, axis):
    blocks = lax.all_gather(shard, axis).astype(jnp.float32)
    return blocks.sum(axis=0)


def together(arrays, axis):
    ends = [0]
    for a in arrays:
        ends.append(ends[-1] + a.size)
    total = lax.psum(jnp.concatenate([a.ravel() for a in arrays]), axis)
    return tuple((total[b:e].reshape(a.shape) for a, b, e in zip(arrays, ends, ends[1:])))


def side_by_side(arrays, axis, dim, along):
    widths = [a.shape[along] for a in arrays]
    both = jnp.concatenate(arrays, axis=along)
    whole = lax.psum_scatter(both, axis, scatter_dimension=dim, tiled=True)
    return tuple(jnp.split(whole, [sum(widths[:k]) for k in range(1, len(widths))], axis=along))


def one_axis_at_a_time(shard, axes):
    return functools.reduce(lax.psum, axes, shard)


def inverse_rms(values):
    return lax.rsqrt(jnp.mean(values * values, axis=-1, keepdims=True) + EPSILON)


def contract_rows(left, right):
    return lax.dot_general(
        left, right, (((0,), (0,)), ((), ())), preferred_element_type=jnp.float32
    )


def contract_cols(left, right):
    return lax.dot_general(
        left, right, (((1,), (1,)), ((), ())), preferred_element_type=jnp.float32
    )


def per_device(
    teacher_in,
    teacher_gain,
    t_gate,
    t_up,
    t_down,
    student_in,
    student_gain,
    s_gate,
    s_up,
    s_down,
    proj,
    layer_map,
):
    tensor_count = lax.axis_size(TENSOR)
    tensor_pos = lax.axis_index(TENSOR)
    token_count = teacher_in.shape[0]
    own_rows = token_count // tensor_count
    row_start = tensor_pos * own_rows
    state = teacher_in
    own_states = []
    full_states = []
    for k in range(T_LAYERS):
        state_wide = state.astype(jnp.float32)
        normed = (state_wide * inverse_rms(state_wide) * teacher_gain[k]).astype(jnp.bfloat16)
        pieces = sent_together((t_gate[k], t_up[k]), DP, 0, 1)
        gate_act = jnp.dot(normed, pieces[0], preferred_element_type=jnp.float32)
        up_act = jnp.dot(normed, pieces[1], preferred_element_type=jnp.float32)
        hidden = (jax.nn.silu(gate_act) * up_act).astype(jnp.bfloat16)
        down_full = gather_axes(t_down[k], DP, 1)
        summed = sum_at_owner(
            jnp.dot(hidden, down_full, preferred_element_type=jnp.float32).astype(jnp.bfloat16),
            TENSOR,
            0,
        )
        residual = lax.dynamic_slice_in_dim(state_wide, row_start, own_rows, 0)
        own_new = (residual + summed).astype(jnp.bfloat16)
        state = gathered_copies(own_new, TENSOR, 0)
        own_states.append(own_new)
        full_states.append(state)
    col_width = proj.shape[1]
    col_start = tensor_pos * col_width
    targets = jnp.stack(
        [lax.dynamic_slice_in_dim(full, col_start, col_width, 1) for full in full_states]
    )
    states = [student_in]
    normeds, gates, ups, units, scales = ([], [], [], [], [])
    for l in range(S_LAYERS):
        wide = states[l].astype(jnp.float32)
        scale = inverse_rms(wide)
        normed = (wide * scale * student_gain[l]).astype(jnp.bfloat16)
        gate_act = jnp.dot(normed, s_gate[l], preferred_element_type=jnp.float32)
        up_act = jnp.dot(normed, s_up[l], preferred_element_type=jnp.float32)
        units_now = (jax.nn.silu(gate_act) * up_act).astype(jnp.bfloat16)
        down_now = s_down[l]
        partial_out = jnp.dot(units_now, down_now, preferred_element_type=jnp.float32)
        result = wide + lax.psum(partial_out.astype(jnp.bfloat16), TENSOR).astype(jnp.float32)
        states.append(result.astype(jnp.bfloat16))
        normeds.append(normed)
        gates.append(gate_act)
        ups.append(up_act)
        units.append(units_now)
        scales.append(scale)
    error_parts = []
    deltas = []
    for l in range(S_LAYERS):
        predicted = jnp.dot(states[l + 1], proj, preferred_element_type=jnp.float32)
        target = lax.dynamic_index_in_dim(targets, layer_map[l], 0, keepdims=False).astype(
            jnp.float32
        )
        errors = predicted - target
        error_parts.append(jnp.sum(errors * errors))
        deltas.append((errors * (2.0 / (S_LAYERS * SEQ))).astype(jnp.bfloat16))
    error_local = jnp.stack(error_parts)
    grad_x = total_of_pieces(
        contract_cols(deltas[S_LAYERS - 1], proj).astype(jnp.bfloat16), TENSOR
    ).astype(jnp.float32)
    gate_grads = [None] * S_LAYERS
    up_grads = [None] * S_LAYERS
    down_grads = [None] * S_LAYERS
    for l in reversed(range(S_LAYERS)):
        grad_out = grad_x.astype(jnp.bfloat16)
        grad_units = contract_cols(grad_out, s_down[l])
        sigma = jax.nn.sigmoid(gates[l])
        grad_gate_act = (grad_units * ups[l] * sigma * (1.0 + gates[l] * (1.0 - sigma))).astype(
            jnp.bfloat16
        )
        grad_up_act = (grad_units * jax.nn.silu(gates[l])).astype(jnp.bfloat16)
        gate_grads[l] = contract_rows(normeds[l], grad_gate_act)
        up_grads[l] = contract_rows(normeds[l], grad_up_act)
        down_grads[l] = contract_rows(units[l], grad_out)
        if l > 0:
            norm_part = contract_cols(grad_gate_act, s_gate[l]) + contract_cols(
                grad_up_act, s_up[l]
            )
            proj_part = contract_cols(deltas[l - 1], proj)
            grad_norm, grad_side = tuple(
                (
                    part.astype(jnp.float32)
                    for part in together(
                        (norm_part.astype(jnp.bfloat16), proj_part.astype(jnp.bfloat16)), TENSOR
                    )
                )
            )
            wide = states[l].astype(jnp.float32)
            scaled = grad_norm * student_gain[l]
            through = scales[l] * scaled - wide * scales[l] ** 3 * jnp.mean(
                wide * scaled, axis=-1, keepdims=True
            )
            grad_x = grad_x + through + grad_side
    proj_local = contract_rows(states[1], deltas[0])
    l = 1
    proj_local = proj_local + contract_rows(states[l + 1], deltas[l])
    grad_gate, grad_up, grad_down, grad_proj = (
        *tuple(
            (
                part.astype(jnp.float32)
                for part in side_by_side(
                    (
                        jnp.stack(gate_grads).astype(jnp.bfloat16),
                        jnp.stack(up_grads).astype(jnp.bfloat16),
                    ),
                    DP,
                    1,
                    0,
                )
            )
        ),
        lax.psum_scatter(
            jnp.stack(down_grads).astype(jnp.bfloat16), DP, scatter_dimension=2, tiled=True
        ).astype(jnp.float32),
        lax.psum_scatter(
            proj_local.astype(jnp.bfloat16), DP, scatter_dimension=0, tiled=True
        ).astype(jnp.float32),
    )
    squares = jnp.stack(
        [
            jnp.sum(grad_gate * grad_gate),
            jnp.sum(grad_up * grad_up),
            jnp.sum(grad_down * grad_down),
            jnp.sum(grad_proj * grad_proj),
        ]
    )
    error_total, square_total = (
        one_axis_at_a_time(error_local, DP_TENSOR),
        one_axis_at_a_time(squares, DP_TENSOR),
    )
    counts = jnp.array(
        [S_LAYERS * DS * FS, S_LAYERS * DS * FS, S_LAYERS * DS * FS, DS * DT], jnp.float32
    )
    mean_error = error_total / (token_count * lax.axis_size(DP) * DT)
    grad_rms = jnp.sqrt(square_total / counts)
    return (jnp.stack(own_states), grad_gate, grad_up, grad_down, grad_proj, mean_error, grad_rms)


def solution(mesh):
    finer = Mesh(mesh.devices.reshape(4, 4, 4, 2), ("dp_0", "dp_1", "tensor_0", "tensor_1"))
    placed = (
        P(DP, None),
        P(),
        P(None, DP, TENSOR),
        P(None, DP, TENSOR),
        P(None, TENSOR, DP),
        P(DP, None),
        P(),
        P(None, None, TENSOR),
        P(None, None, TENSOR),
        P(None, TENSOR, None),
        P(None, TENSOR),
        P(),
    )
    return jax.shard_map(
        per_device,
        mesh=finer,
        in_specs=placed,
        out_specs=(
            P(None, DP_TENSOR, None),
            P(None, DP, TENSOR),
            P(None, DP, TENSOR),
            P(None, TENSOR, DP),
            P(DP, TENSOR),
            P(),
            P(),
        ),
        check_vma=False,
    )
```

profile of v0, /device:TPU:1, one launch (start us, length us, event | category | flops | bytes accessed | tf_op | source)
XLA Modules:
  0.0 663.2 jit_solution(12386800361999431912)
XLA Ops:
  8.1 1.8 fusion.127
  9.8 1.8 fusion.128
  13.0 15.8 %all-gather = bf16[1,684,512]{2,1,0:T(8,128)(2,1)} all-gather(bf16[1,684,128]{2,1,0:T(8,128)(2,1)S(1)} %copy.40), channel_id=2, replica_groups=mesh['dp_0'=4,'dp_1'=4,'tensor_0'=4,'tensor_1'=2] {'dp_1'}, dimensions={2}, use_global_device_ids=true | all-gather | bytes 875520 | tf_op jit(solution)/shard_map/all_gather | solution.py:34
  29.0 0.8 pad_maximum_fusion.4
  29.9 17.2 %all-gather.2 = bf16[1,684,512]{2,1,0:T(8,128)(2,1)} all-gather(bf16[1,684,128]{2,1,0:T(8,128)(2,1)S(1)} %copy.43), channel_id=4, replica_groups=mesh['dp_0'=4,'dp_1'=4,'tensor_0'=4,'tensor_1'=2] {'dp_1'}, dimensions={2}, use_global_device_ids=true | all-gather | bytes 875520 | tf_op jit(solution)/shard_map/all_gather | solution.py:34
  47.5 32.9 %all-gather.11.cloned.1.call-done = bf16[2048,1368]{0,1:T(8,128)(2,1)} async-done(((bf16[128,1368]{0,1:T(8,128)(2,1)}), bf16[2048,1368]{0,1:T(8,128)(2,1)}) %all-gather.11.cloned.1.call-update) | async-done | bytes 5603344 | tf_op jit(solution)/shard_map/all_gather | solution.py:25
  80.4 2.8 fusion.6
  83.2 36.3 %all-gather.15.cloned.1.call-done = bf16[1,684,2048]{2,1,0:T(8,128)(2,1)} async-done(((bf16[1,684,512]{2,1,0:T(8,128)(2,1)}), bf16[1,684,2048]{2,1,0:T(8,128)(2,1)}) %all-gather.15.cloned.1.call-update) | async-done | bytes 2801680 | tf_op jit(solution)/shard_map/all_gather | solution.py:34
  119.5 7.0 %fusion.12 = bf16[256,2048]{1,0:T(8,128)(2,1)} fusion(bf16[1,684,2048]{2,1,0:T(8,128)(2,1)} %all-gather.15.cloned.1.call-done, bf16[2048,1368]{0,1:T(8,128)(2,1)} %all-gather.11.cloned.1.call-done, f32[256,684]{0,1:T(8,128)S(1)} %fusion.6, f32[2048]{0:T(1024)S(1)} %bitcast.140, f32[256]{0:T(256)S(1)} %add_rsqrt_fusion.3, bf16[256,2048]{1,0:T(8,128)(2,1)S(1)} %copy-done.2), kind=kOutput, calls=%fused_computation.14 | convolution fusion | flops 1438124032 | bytes 8442880 | tf_op jit(solution)/shard_map/dot_general | solution.py:135
  126.4 5.3 all-to-all-start
  131.7 1.6 convert_element_type.154
  133.5 13.2 %all-to-all-done = bf16[8,32,2048]{2,1,0:T(8,128)(2,1)S(1)} async-done(((bf16[8,32,2048]{2,1,0:T(8,128)(2,1)}), bf16[8,32,2048]{2,1,0:T(8,128)(2,1)S(1)}, u32[]{:S(2)}, u32[]{:S(2)}) %all-to-all-start) | async-done | bytes 1048608 | tf_op jit(solution)/shard_map/all_to_all | solution.py:45
  146.8 1.0 add_convert_fusion.1
  147.8 1.1 broadcast_in_dim.4
  148.9 4.4 all-to-all-start.1
  153.4 1.8 fusion.69
  155.3 1.4 multiply_convert_fusion.7
  157.3 1.2 convolution_convert_fusion.9
  158.6 9.7 %all-to-all-done.1 = bf16[8,32,2048]{2,1,0:T(8,128)(2,1)S(1)} async-done(((bf16[8,32,2048]{2,1,0:T(8,128)(2,1)}), bf16[8,32,2048]{2,1,0:T(8,128)(2,1)S(1)}, u32[]{:S(2)}, u32[]{:S(2)}) %all-to-all-start.1) | async-done | bytes 1048608 | tf_op jit(solution)/shard_map/all_to_all | solution.py:57
  168.7 15.3 %all-gather.13.cloned.1.call-done = bf16[2048,1368]{0,1:T(8,128)(2,1)} async-done(((bf16[128,1368]{0,1:T(8,128)(2,1)}), bf16[2048,1368]{0,1:T(8,128)(2,1)}) %all-gather.13.cloned.1.call-update) | async-done | bytes 5603344 | tf_op jit(solution)/shard_map/all_gather | solution.py:25
  184.0 2.8 fusion.2
  186.8 36.2 %all-gather.17.cloned.1.call-done = bf16[1,684,2048]{2,1,0:T(8,128)(2,1)} async-done(((bf16[1,684,512]{2,1,0:T(8,128)(2,1)}), bf16[1,684,2048]{2,1,0:T(8,128)(2,1)}) %all-gather.17.cloned.1.call-update) | async-done | bytes 2801680 | tf_op jit(solution)/shard_map/all_gather | solution.py:34
  223.1 7.0 %fusion.15 = bf16[256,2048]{1,0:T(8,128)(2,1)} fusion(bf16[1,684,2048]{2,1,0:T(8,128)(2,1)} %all-gather.17.cloned.1.call-done, bf16[2048,1368]{0,1:T(8,128)(2,1)} %all-gather.13.cloned.1.call-done, f32[256,684]{0,1:T(8,128)S(1)} %fusion.2, f32[2048]{0:T(1024)S(1)} %bitcast.138, f32[256]{0:T(256)S(1)} %rsqrt.40, bf16[256,2048]{1,0:T(8,128)(2,1)S(1)} %bitcast.121), kind=kOutput, calls=%fused_computation.15 | convolution fusion | flops 1438124032 | bytes 8442880 | tf_op jit(solution)/shard_map/dot_general | solution.py:135
  230.0 5.3 all-to-all-start.2
  235.3 1.5 fusion.44
  236.8 1.7 bitcast_convert_fusion
  238.4 11.8 %all-to-all-done.2 = bf16[8,32,2048]{2,1,0:T(8,128)(2,1)S(1)} async-done(((bf16[8,32,2048]{2,1,0:T(8,128)(2,1)}), bf16[8,32,2048]{2,1,0:T(8,128)(2,1)S(1)}, u32[]{:S(2)}, u32[]{:S(2)}) %all-to-all-start.2) | async-done | bytes 1048608 | tf_op jit(solution)/shard_map/all_to_all | solution.py:45
  250.4 1.0 add_convert_fusion
  251.4 1.1 broadcast_in_dim.5
  252.5 4.4 all-to-all-start.3
  256.9 1.9 fusion.62
  258.9 1.3 multiply_convert_fusion.6
  260.8 1.2 convolution_convert_fusion.8
  264.7 7.2 %all-to-all-done.3 = bf16[8,32,2048]{2,1,0:T(8,128)(2,1)S(1)} async-done(((bf16[8,32,2048]{2,1,0:T(8,128)(2,1)}), bf16[8,32,2048]{2,1,0:T(8,128)(2,1)S(1)}, u32[]{:S(2)}, u32[]{:S(2)}) %all-to-all-start.3) | async-done | bytes 1048608 | tf_op jit(solution)/shard_map/all_to_all | solution.py:57
  272.0 48.9 %all-reduce.12.cloned.1.call-done = bf16[256,1024]{1,0:T(8,128)(2,1)} async-done(((bf16[256,1024]{1,0:T(8,128)(2,1)}), bf16[256,1024]{1,0:T(8,128)(2,1)}) %all-reduce.12.cloned.1.call-update) | async-done | bytes 524304 | tf_op jit(solution)/shard_map/psum | solution.py:160
  320.9 2.0 multiply_reduce_fusion.5
  322.8 1.1 convolution_convert_fusion.7
  326.0 0.9 multiply_reduce_fusion.6
  327.3 30.4 %all-gather.19.cloned.1.call-done = bf16[2048,1024]{1,0:T(8,128)(2,1)} async-done(((bf16[256,1024]{1,0:T(8,128)(2,1)}), bf16[2048,1024]{1,0:T(8,128)(2,1)}) %all-gather.19.cloned.1.call-update) | async-done | bytes 4194320 | tf_op jit(solution)/shard_map/all_gather | solution.py:65
  357.7 3.3 convert_reduce_fusion
  361.7 1.0 copy-done.13
  364.2 1.1 pad_maximum_fusion.2
  365.8 1.2 fusion.25
  367.2 1.5 fusion.23
  368.7 57.0 %all-reduce.14.cloned.1.call-done = bf16[524288]{0:T(1024)(128)(2,1)} async-done(((bf16[524288]{0:T(1024)(128)(2,1)}), bf16[524288]{0:T(1024)(128)(2,1)}) %all-reduce.14.cloned.1.call-update) | async-done | bytes 1048592 | tf_op jit(solution)/shard_map/psum | solution.py:73
  425.6 2.7 slice_convert_fusion.1
  428.3 1.4 reshape.117
  429.7 2.3 reshape.118
  432.3 1.0 copy-done.3
  434.9 4.1 copy.36
  439.0 0.9 copy-done.10
  443.8 2.3 pad_maximum_fusion
  448.7 1.4 pad_maximum_fusion.6
  450.0 2.0 multiply_reduce_fusion.7
  452.0 81.9 %all-reduce.16.cloned.1.call-done = bf16[2,512,1024]{1,0,2:T(2,128)(2,1)} async-done(((bf16[2,512,1024]{1,0,2:T(2,128)(2,1)}), bf16[2,512,1024]{1,0,2:T(2,128)(2,1)}) %all-reduce.16.cloned.1.call-update) | async-done | bytes 2097168
  534.0 1.8 multiply_reduce_fusion.2
  535.8 1.0 dynamic-slice_convert_fusion
  536.8 78.1 %reduce-scatter.3.cloned.1.call-done = bf16[4,64,512]{2,1,0:T(8,128)(2,1)} async-done(((bf16[4,1024,512]{2,1,0:T(8,128)(2,1)}), bf16[4,64,512]{2,1,0:T(8,128)(2,1)}) %reduce-scatter.3.cloned.1.call-update) | async-done | bytes 262160 | tf_op jit(solution)/shard_map/reduce_scatter | solution.py:80
  614.8 2.4 multiply_reduce_fusion.3
  617.2 2.6 pad_maximum_fusion.7
  620.6 7.3 %all-reduce.3 = (f32[2]{0:T(128)S(1)}, f32[4]{0:T(128)S(1)}) all-reduce(f32[2]{0:T(128)S(1)} %pad_maximum_fusion.6, f32[4]{0:T(128)S(1)} %pad_maximum_fusion.7), channel_id=1, replica_groups=mesh['dp_0'=4,'dp_1'=4,'tensor_0'=4,'tensor_1'=2] {'dp_0'}, use_global_device_ids=true, to_apply=%region_16.17 | all-reduce | flops 6 | bytes 48 | tf_op jit(solution)/shard_map/psum | solution.py:85
  628.0 7.3 %all-reduce.2 = (f32[2]{0:T(128)S(1)}, f32[4]{0:T(128)S(1)}) all-reduce(f32[2]{0:T(128)S(1)} %get-tuple-element.32, f32[4]{0:T(128)S(1)} %get-tuple-element.33), channel_id=1, replica_groups=mesh['dp_0'=4,'dp_1'=4,'tensor_0'=4,'tensor_1'=2] {'dp_1'}, use_global_device_ids=true, to_apply=%region_17.18 | all-reduce | flops 6 | bytes 48 | tf_op jit(solution)/shard_map/psum | solution.py:85
  635.3 8.6 %all-reduce.1 = (f32[2]{0:T(128)S(1)}, f32[4]{0:T(128)S(1)}) all-reduce(f32[2]{0:T(128)S(1)} %get-tuple-element.30, f32[4]{0:T(128)S(1)} %get-tuple-element.31), channel_id=1, replica_groups=mesh['dp_0'=4,'dp_1'=4,'tensor_0'=4,'tensor_1'=2] {'tensor_0'}, use_global_device_ids=true, to_apply=%region_18.19 | all-reduce | flops 6 | bytes 48 | tf_op jit(solution)/shard_map/psum | solution.py:85
  643.9 10.6 %all-reduce.4 = (f32[2]{0:T(128)S(1)}, f32[4]{0:T(128)S(1)}) all-reduce(f32[2]{0:T(128)S(1)} %get-tuple-element.28, f32[4]{0:T(128)S(1)} %get-tuple-element.29), channel_id=1, replica_groups=mesh['dp_0'=4,'dp_1'=4,'tensor_0'=4,'tensor_1'=2] {'tensor_1'}, use_global_device_ids=true, to_apply=%region_19.20 | all-reduce | flops 6 | bytes 48 | tf_op jit(solution)/shard_map/psum | solution.py:85
  (140 shorter events, 17.8 us)
Async XLA Ops:
  8.0 312.9 %copy-start = (bf16[1024,256]{1,0:T(8,128)(2,1)S(1)}, bf16[1024,256]{1,0:T(8,128)(2,1)}, u32[]{:S(2)}) copy-start(bf16[1024,256]{1,0:T(8,128)(2,1)} %param.23) | copy-start | bytes 1572868
  8.0 72.4 %all-gather.11.cloned.1.call-start = ((), (), s32[]{:S(2)}) async-start(), calls=%async_computation.6 | async-start | bytes 5953536 | tf_op jit(solution)/shard_map/all_gather | solution.py:25
  9.8 2.7 copy-start.8
  12.5 107.0 %all-gather.15.cloned.1.call-start = ((), (), s32[]{:S(2)}) async-start(), calls=%async_computation.13 | async-start | bytes 3522560 | tf_op jit(solution)/shard_map/all_gather | solution.py:34
  28.9 155.1 %all-gather.13.cloned.1.call-start = ((), (), s32[]{:S(2)}) async-start(), calls=%async_computation.7 | async-start | bytes 5953536 | tf_op jit(solution)/shard_map/all_gather | solution.py:25
  28.9 18.2 %copy-start.2 = (bf16[256,2048]{1,0:T(8,128)(2,1)S(1)}, bf16[256,2048]{1,0:T(8,128)(2,1)}, u32[]{:S(2)}) copy-start(bf16[256,2048]{1,0:T(8,128)(2,1)} %param.13) | copy-start | bytes 3145732
  29.0 18.4 %copy-start.21 = (f32[2,2048]{1,0:T(2,128)S(1)}, f32[2,2048]{1,0:T(2,128)}, u32[]{:S(2)}) copy-start(f32[2,2048]{1,0:T(2,128)} %param.14) | copy-start | bytes 49156
  29.8 193.2 %all-gather.17.cloned.1.call-start = ((), (), s32[]{:S(2)}) async-start(), calls=%async_computation.14 | async-start | bytes 3522560 | tf_op jit(solution)/shard_map/all_gather | solution.py:34
  126.4 20.2 %all-to-all-start = ((bf16[8,32,2048]{2,1,0:T(8,128)(2,1)}), bf16[8,32,2048]{2,1,0:T(8,128)(2,1)S(1)}, u32[]{:S(2)}, u32[]{:S(2)}) async-start(bf16[8,32,2048]{2,1,0:T(8,128)(2,1)} %bitcast.129), calls=%async_computation | async-start | bytes 2097152 | tf_op jit(solution)/shard_map/all_to_all | solution.py:45
  131.7 1.6 copy-start.5
  131.7 1.7 copy-start.22
  148.9 19.4 %all-to-all-start.1 = ((bf16[8,32,2048]{2,1,0:T(8,128)(2,1)}), bf16[8,32,2048]{2,1,0:T(8,128)(2,1)S(1)}, u32[]{:S(2)}, u32[]{:S(2)}) async-start(bf16[8,32,2048]{2,1,0:T(8,128)(2,1)} %broadcast_in_dim.4), calls=%async_computation.1 | async-start | bytes 2097152 | tf_op jit(solution)/shard_map/all_to_all | solution.py:57
  153.3 82.0 %all-reduce.10.cloned.1.call-start = ((), (), s32[]{:S(2)}) async-start(), calls=%async_computation.8 | async-start | bytes 1048576 | tf_op jit(solution)/shard_map/psum | solution.py:160
  153.3 1.9 copy-start.14
  153.4 3.3 copy-start.24
  155.3 1.4 copy-start.32
  155.3 2.1 copy-start.26
  156.7 30.1 %copy-start.17 = (bf16[256,512]{1,0:T(8,128)(2,1)}, bf16[256,512]{1,0:T(8,128)(2,1)S(1)}, u32[]{:S(2)}) copy-start(bf16[256,512]{1,0:T(8,128)(2,1)S(1)} %get-tuple-element.64) | copy-start | bytes 786436
  230.0 20.2 %all-to-all-start.2 = ((bf16[8,32,2048]{2,1,0:T(8,128)(2,1)}), bf16[8,32,2048]{2,1,0:T(8,128)(2,1)S(1)}, u32[]{:S(2)}, u32[]{:S(2)}) async-start(bf16[8,32,2048]{2,1,0:T(8,128)(2,1)} %bitcast.130), calls=%async_computation.2 | async-start | bytes 2097152 | tf_op jit(solution)/shard_map/all_to_all | solution.py:45
  252.5 19.4 %all-to-all-start.3 = ((bf16[8,32,2048]{2,1,0:T(8,128)(2,1)}), bf16[8,32,2048]{2,1,0:T(8,128)(2,1)S(1)}, u32[]{:S(2)}, u32[]{:S(2)}) async-start(bf16[8,32,2048]{2,1,0:T(8,128)(2,1)} %broadcast_in_dim.5), calls=%async_computation.3 | async-start | bytes 2097152 | tf_op jit(solution)/shard_map/all_to_all | solution.py:57
  256.9 63.9 %all-reduce.12.cloned.1.call-start = ((), (), s32[]{:S(2)}) async-start(), calls=%async_computation.9 | async-start | bytes 1048576 | tf_op jit(solution)/shard_map/psum | solution.py:160
  256.9 1.9 copy-start.15
  258.8 1.3 copy-start.34
  258.9 2.0 copy-start.27
  260.1 0.7 copy-start.19
  260.1 2.0 copy-start.23
  262.1 95.6 %all-gather.19.cloned.1.call-start = ((), (), s32[]{:S(2)}) async-start(), calls=%async_computation.15 | async-start | bytes 4718592 | tf_op jit(solution)/shard_map/all_gather | solution.py:65
  324.0 101.6 %all-reduce.14.cloned.1.call-start = ((), (), s32[]{:S(2)}) async-start(), calls=%async_computation.10 | async-start | bytes 2097152 | tf_op jit(solution)/shard_map/psum | solution.py:73
  357.7 3.3 copy-start.28
  357.7 3.3 copy-start.35
  357.7 3.3 copy-start.37
  361.1 1.6 copy-start.13
  361.7 2.4 copy-start.9
  361.7 2.4 copy-start.11
  361.7 1.9 copy-start.16
  364.2 1.5 copy-start.7
  365.3 84.7 %reduce-scatter.5.cloned.1.call-start = ((), (), s32[]{:S(2)}) async-start(), calls=%async_computation.12 | async-start | bytes 557056 | tf_op jit(solution)/shard_map/reduce_scatter | solution.py:235
  365.7 1.5 copy-start.20
  366.9 167.0 %all-reduce.16.cloned.1.call-start = ((), (), s32[]{:S(2)}) async-start(), calls=%async_computation.16 | async-start | bytes 4194304
  432.0 1.2 copy-start.3
  433.3 1.0 copy-start.18
  433.3 1.4 copy-start.4
  439.0 1.0 copy-start.10
  439.0 1.5 copy-start.12
  439.0 175.8 %reduce-scatter.3.cloned.1.call-start = ((), (), s32[]{:S(2)}) async-start(), calls=%async_computation.11 | async-start | bytes 4456448 | tf_op jit(solution)/shard_map/reduce_scatter | solution.py:80
  439.9 1.6 copy-start.29
  440.5 1.5 copy-start.6
  440.5 1.5 copy-start.25
  440.5 1.5 copy-start.33
  442.0 1.0 copy-start.36
  446.1 0.7 copy-start.31
  446.1 209.0 %copy-start.30 = (f32[4]{0:T(128)S(1)}, f32[4]{0:T(128)}, u32[]{:S(2)}) copy-start(f32[4]{0:T(128)} %constant.58) | copy-start | bytes 52
  446.1 209.5 %copy-start.1 = (bf16[1024,256]{1,0:T(8,128)(2,1)S(1)}, bf16[1024,256]{1,0:T(8,128)(2,1)}, u32[]{:S(2)}) copy-start(bf16[1024,256]{1,0:T(8,128)(2,1)} %param.23) | copy-start | bytes 1572868
Sparse Core Ops, SparseCore 0:
  12.6 67.7 all-gather.10
  82.0 37.3 all-gather.14
  121.6 62.3 all-gather.12
  185.5 37.5 all-gather.16
  369.0 71.0 reduce-scatter.4
  443.3 90.6 all-reduce.15
  537.3 77.4 reduce-scatter.2
Sparse Core Ops, SparseCore 1:
  158.7 59.6 all-reduce.9
  262.2 58.6 all-reduce.11
  324.1 33.6 all-gather.18
  365.4 60.2 all-reduce.13
where the time goes:
time: 664 us; the launch traced here: 663 us
  waiting for transfers between devices  459 us (69%)
  blocking collectives  66.9 us (10%)
  matrix products  40.5 us (6%)
  other arithmetic  32.4 us (5%)
  local copies, waits for them, and re-layouts  23.4 us (4%)
  between operations  20.9 us (3%)
  starting transfers between devices  20 us (3%)
    unnamed x12, waiting for transfers between devices  82.1 us
    reduce_scatter x1, waiting for transfers between devices, side_by_side(): whole = lax.psum_scatter(both, axis, scatter_dimension=dim, tiled=True)  78.1 us
    all_gather x2, waiting for transfers between devices, gather_axes(): shard = lax.all_gather(shard, axis, axis=dim, tiled=True)  72.5 us
    psum x1, waiting for transfers between devices, together(): total = lax.psum(jnp.concatenate([a.ravel() for a in arrays]), axis)  57 us
    psum x2, waiting for transfers between devices, per_device(): lax.psum(partial_out.astype(jnp.bfloat16), TENSOR).astype(jnp.float32)  48.9 us
    all_gather x2, waiting for transfers between devices, sent_together(): lax.all_gather(both, axis, axis=dim, tiled=True)  48.2 us
    psum x4, blocking collectives, one_axis_at_a_time(): return functools.reduce(lax.psum, axes, shard)  33.9 us
    all_gather x2, blocking collectives, gather_axes(): shard = lax.all_gather(shard, axis, axis=dim, tiled=True)  33 us
  transfers between devices with their start and end apart: 15, of which 13 were waited for; matrix products, arithmetic and copies ran while one was open for 10% of the time, Pallas kernels for 0%

commit v1 on v0

v1 whole, which is shorter than its diff:
```python
import functools

import jax
import jax.numpy as jnp
from jax import lax
from jax.experimental import pallas as pl
from jax.experimental.pallas import tpu as pltpu
from jax.sharding import Mesh
from jax.sharding import PartitionSpec as P

DT = 2048
DS = 1024
FS = 4096
T_LAYERS = 2
S_LAYERS = 2
SEQ = 512
TENSOR = ("tensor_0", "tensor_1")
DP = ("dp_0", "dp_1")
DP_TENSOR = ("dp_0", "dp_1", "tensor_0", "tensor_1")
EPSILON = 1e-05
MESH = pl.DeviceIdType.MESH
BF = jnp.bfloat16
F32 = jnp.float32
N_COPY = 104
N_LOCAL = 9
GU_HALVES = ((0, 32, 64), (64, 96, 128))
DN_HALVES = ((0, 176, 352), (352, 512, 688))
VMEM = pltpu.VMEM


def dot(a, b):
    return jnp.dot(a, b, preferred_element_type=F32)


def contract_rows(left, right):
    return lax.dot_general(left, right, (((0,), (0,)), ((), ())), preferred_element_type=F32)


def contract_cols(left, right):
    return lax.dot_general(left, right, (((1,), (1,)), ((), ())), preferred_element_type=F32)


def inverse_rms(values):
    return lax.rsqrt(jnp.mean(values * values, axis=-1, keepdims=True) + EPSILON)


def silu(v):
    return v / (1.0 + jnp.exp(-v))


def loop(count, step, body):
    def once(i, carry):
        body(pl.multiple_of(i * step, step))
        return carry

    lax.fori_loop(0, count // step, once, 0)


class Copies:
    def __init__(self, send, recv):
        self.send, self.recv, self.used, self.made = send, recv, 0, []

    def tags(self, count):
        first = self.used
        self.used += count
        return list(range(first, first + count))

    def start(self, tag, src, dst, where):
        copy = pltpu.make_async_remote_copy(
            src_ref=src,
            dst_ref=dst,
            send_sem=self.send.at[tag],
            recv_sem=self.recv.at[tag],
            device_id=where,
            device_id_type=MESH,
        )
        copy.start()
        self.made.append(copy)
        return copy

    def finish(self):
        for copy in self.made:
            copy.wait_send()


class Gather:
    def __init__(self, copies, buf, halves, y, x):
        self.c, self.buf, self.halves, self.y, self.x = copies, buf, halves, y, x

    def slab(self, half, outer, inner, lo, hi):
        r = pl.ds(lo, hi - lo)
        return self.buf.at[outer, inner, r] if half == 0 else self.buf.at[inner, outer, r]

    def axes(self, half):
        if half == 0:
            return "dp_1", self.x, "dp_0", self.y
        return "dp_0", self.y, "dp_1", self.x

    def first(self):
        self.own = []
        for half in (0, 1):
            a, pa, _, pb = self.axes(half)
            lo, _, hi = self.halves[half]
            mine = self.slab(half, pb, pa, lo, hi)
            t = self.c.tags(2)
            self.own.append(
                (
                    self.c.start(t[0], mine, mine, {a: lax.rem(pa + 1, 4)}),
                    self.c.start(t[1], mine, mine, {a: lax.rem(pa + 3, 4)}),
                )
            )

    def first_forward(self):
        self.fwd = []
        for half in (0, 1):
            a, pa, _, pb = self.axes(half)
            lo, mid, hi = self.halves[half]
            up, down = lax.rem(pa + 1, 4), lax.rem(pa + 3, 4)
            t = self.c.tags(2)
            self.own[half][0].wait_recv()
            piece = self.slab(half, pb, down, lo, mid)
            f0 = self.c.start(t[0], piece, piece, {a: up})
            self.own[half][1].wait_recv()
            piece = self.slab(half, pb, up, mid, hi)
            f1 = self.c.start(t[1], piece, piece, {a: down})
            self.fwd.append((f0, f1))

    def second(self):
        self.row = []
        for half in (0, 1):
            _, _, b, pb = self.axes(half)
            lo, _, hi = self.halves[half]
            self.fwd[half][0].wait_recv()
            self.fwd[half][1].wait_recv()
            t = self.c.tags(2)
            mine = self.slab(half, pb, pl.ds(0, 4), lo, hi)
            self.row.append(
                (
                    self.c.start(t[0], mine, mine, {b: lax.rem(pb + 1, 4)}),
                    self.c.start(t[1], mine, mine, {b: lax.rem(pb + 3, 4)}),
                )
            )

    def second_forward(self):
        self.last = []
        for half in (0, 1):
            _, _, b, pb = self.axes(half)
            lo, _, hi = self.halves[half]
            up, down = lax.rem(pb + 1, 4), lax.rem(pb + 3, 4)
            t = self.c.tags(2)
            self.row[half][0].wait_recv()
            piece = self.slab(half, down, pl.ds(0, 2), lo, hi)
            f0 = self.c.start(t[0], piece, piece, {b: up})
            self.row[half][1].wait_recv()
            piece = self.slab(half, up, pl.ds(2, 2), lo, hi)
            f1 = self.c.start(t[1], piece, piece, {b: down})
            self.last.append((f0, f1))

    def complete(self):
        for pair in self.last:
            for copy in pair:
                copy.wait_recv()


class TensorSum:
    def __init__(self, copies, part, pair, both, ring, z, c):
        self.c, self.part, self.pair, self.both, self.ring = copies, part, pair, both, ring
        self.z, self.core = z, c

    def across(self):
        other = 1 - self.core
        self.x = self.c.start(self.c.tags(1)[0], self.part.at[other], self.pair, {"tensor_1": other})

    def along(self):
        self.x.wait_recv()
        rows = self.part.shape[2]
        for k in range(4):
            self.both[k] = (self.part[self.core, k].astype(F32) + self.pair[k].astype(F32)).astype(BF)
        self.s = []
        for k in (2, 1, 3):
            to = lax.rem(self.z + k, 4)
            self.s.append(
                self.c.start(self.c.tags(1)[0], self.both.at[to], self.ring.at[self.z], {"tensor_0": to})
            )

    def total(self):
        for copy in self.s:
            copy.wait_recv()
        acc = self.both[self.z].astype(F32)
        for k in (1, 2, 3):
            acc = acc + self.ring[lax.rem(self.z + k, 4)].astype(F32)
        return acc


class TensorGather:
    def __init__(self, copies, buf, z, c):
        self.c, self.buf, self.z, self.core = copies, buf, z, c

    def along(self):
        self.s = []
        for k in (2, 1, 3):
            mine = self.buf.at[self.core, self.z]
            to = lax.rem(self.z + k, 4)
            self.s.append(self.c.start(self.c.tags(1)[0], mine, mine, {"tensor_0": to}))

    def across(self):
        for copy in self.s:
            copy.wait_recv()
        mine = self.buf.at[self.core]
        self.x = self.c.start(self.c.tags(1)[0], mine, mine, {"tensor_1": 1 - self.core})

    def complete(self):
        self.x.wait_recv()


def blocks(ref, *lead, rows=slice(None)):
    return jnp.concatenate([ref[lead + (t % 2, t // 2, rows)] for t in range(8)], axis=1)


def forward_kernel(
    tin, tgain, sin, sgain, gu_in, dn_in, sg_in, su_in, sd_in,
    states_out, target_out, x_out, sn_out, a_out, b_out, u_out,
    wg, wd, sg, su, sd, xs, tn, acts, hid, sn,
    spart, spair, sboth, sring, tpart, tpair, tboth, tring, hn, rows_in,
    send, recv, local,
):
    y, x = lax.axis_index("dp_0"), lax.axis_index("dp_1")
    z, c = lax.axis_index("tensor_0"), lax.axis_index("tensor_1")
    t = 2 * z + c
    peers = [{"dp_0": lax.rem(y + k, 4)} for k in (1, 3)]
    peers += [{"dp_1": lax.rem(x + k, 4)} for k in (1, 3)]
    others = [lax.rem(t + k, 8) for k in range(1, 8)]
    peers += [{"tensor_0": o // 2, "tensor_1": lax.rem(o, 2)} for o in others]
    barrier = pltpu.get_barrier_semaphore()
    for peer in peers:
        pl.semaphore_signal(barrier, inc=1, device_id=peer, device_id_type=MESH)
    copies = Copies(send, recv)

    loads = []

    def load(src, dst):
        copy = pltpu.make_async_copy(src, dst, local.at[len(loads)])
        copy.start()
        loads.append(copy)

    for l in (0, 1):
        load(gu_in.at[l], wg.at[l, y, x])
        load(dn_in.at[l], wd.at[l, y, x])
    load(sg_in, sg)
    load(su_in, su)
    load(sd_in, sd)
    gu = [Gather(copies, wg.at[l], GU_HALVES, y, x) for l in (0, 1)]
    dn = [Gather(copies, wd.at[l], DN_HALVES, y, x) for l in (0, 1)]
    pl.semaphore_wait(barrier, len(peers))
    loads[0].wait()
    gu[0].first()
    loads[1].wait()
    dn[0].first()

    def teacher_norm(k):
        def body(r):
            rows = pl.ds(r, 32)
            h = tin[rows, :].astype(F32) if k == 0 else blocks(hn, 0, rows=rows).astype(F32)
            tn[rows, :] = (h * inverse_rms(h) * tgain[k:k + 1, :]).astype(BF)

        loop(256, 32, body)

    def student_norm(l):
        def body(r):
            rows = pl.ds(r, 64)
            v = sin[rows, :].astype(F32) if l == 0 else blocks(xs, 0, rows=rows).astype(F32)
            sn[l, rows, :] = (v * inverse_rms(v) * sgain[l:l + 1, :]).astype(BF)

        loop(256, 64, body)

    def student_units(l):
        def body(n):
            cols = pl.ds(n, 256)
            a = dot(sn[l], sg[l, :, cols])
            b = dot(sn[l], su[l, :, cols])
            a_out[l, :, cols] = a
            b_out[l, :, cols] = b
            u_out[l, :, cols] = (silu(a) * b).astype(BF)

        loop(512, 256, body)

    def student_part(l):
        def body(i, carry):
            p = dot(u_out[l], sd[l, :, pl.ds(pl.multiple_of(i * 256, 256), 256)])
            spart[l, 0, i] = p[:, :128].astype(BF)
            spart[l, 1, i] = p[:, 128:].astype(BF)
            return carry

        lax.fori_loop(0, 4, body, 0)

    def teacher_up(k):
        def body(n):
            cols = pl.ds(n, 256)
            w = wg[k, :, :, :, cols].reshape(DT, 256)
            acts[:, cols] = dot(tn[...], w)

        loop(1280, 256, body)
        acts[:, 1280:1408] = dot(tn[...], wg[k, :, :, :, 1280:1408].reshape(DT, 128))

        def unit(r):
            rows = pl.ds(r, 32)
            hid[rows, 0:640] = (silu(acts[rows, 0:640]) * acts[rows, 640:1280]).astype(BF)
            tail = acts[rows, 1280:1408]
            hid[rows, 640:768] = (silu(tail) * pltpu.roll(tail, 64, 1)).astype(BF)

        loop(256, 32, unit)

    def teacher_down(k):
        def body(i, carry):
            q = 2 * lax.rem(i, 2)
            w = jnp.concatenate([wd[k, i // 2, q], wd[k, i // 2, q + 1]], axis=1)
            tpart[k, lax.rem(i, 2), i // 2] = dot(hid[:, 0:688], w).astype(BF)
            return carry

        lax.fori_loop(0, 8, body, 0)

    ssum = [TensorSum(copies, spart.at[l], spair.at[l], sboth.at[l], sring.at[l], z, c) for l in (0, 1)]
    sgather = [TensorGather(copies, xs.at[l], z, c) for l in (0, 1)]
    tsum = [TensorSum(copies, tpart.at[k], tpair.at[k], tboth.at[k], tring.at[k], z, c) for k in (0, 1)]
    tgather = TensorGather(copies, hn.at[0], z, c)

    def student_result(l):
        if l == 0:
            old = sin[:, pl.ds(pl.multiple_of(t * 128, 128), 128)]
        else:
            old = xs[0, c, z]
        xs[l, c, z] = (old.astype(F32) + ssum[l].total()).astype(BF)

    def teacher_result(k):
        if k == 0:
            old = tin[:, pl.ds(pl.multiple_of(t * 256, 256), 256)]
        else:
            old = hn[0, c, z]
        new = (old.astype(F32) + tsum[k].total()).astype(BF)
        hn[k, c, z] = new
        target_out[k] = new

    def student(l):
        student_norm(l)
        if l == 0:
            for copy in loads[4:7]:
                copy.wait()
        student_units(l)
        student_part(l)
        ssum[l].across()

    def student_end(l):
        ssum[l].along()
        student_result(l)
        sgather[l].along()
        sgather[l].across()
        sgather[l].complete()

    teacher_norm(0)
    gu[0].first_forward()
    dn[0].first_forward()
    gu[0].second()
    loads[2].wait()
    gu[1].first()
    student(0)
    dn[0].second()
    student_end(0)
    gu[0].second_forward()
    gu[1].first_forward()
    student(1)
    student_end(1)
    dn[0].second_forward()
    gu[1].second()
    loads[3].wait()
    dn[1].first()
    gu[0].complete()
    teacher_up(0)
    dn[0].complete()
    teacher_down(0)
    tsum[0].across()
    dn[1].first_forward()
    tsum[0].along()
    teacher_result(0)
    tgather.along()
    dn[1].second()
    tgather.across()
    tgather.complete()
    teacher_norm(1)
    gu[1].second_forward()
    x_out[...] = xs[...]
    sn_out[...] = sn[...]
    for i in range(8):
        states_out[0, :, i * 256:(i + 1) * 256] = hn[0, i % 2, i // 2, pl.ds(pl.multiple_of(t * 32, 32), 32), :]
    dn[1].second_forward()
    gu[1].complete()
    teacher_up(1)
    dn[1].complete()
    teacher_down(1)
    tsum[1].across()
    tsum[1].along()
    teacher_result(1)
    shared = []
    for o in others:
        rows = pl.ds(pl.multiple_of(o * 32, 32), 32)
        where = {"tensor_0": o // 2, "tensor_1": lax.rem(o, 2)}
        shared.append(copies.start(copies.tags(1)[0], hn.at[1, c, z, rows], rows_in.at[t], where))
    rows_in[t] = hn[1, c, z, pl.ds(pl.multiple_of(t * 32, 32), 32), :]
    for copy in shared:
        copy.wait_recv()
    for i in range(8):
        states_out[1, :, i * 256:(i + 1) * 256] = rows_in[i]
    copies.finish()


def run_forward(tin, tgain, sin, sgain, gu, dn, sg, su, sd):
    shape = jax.ShapeDtypeStruct
    here = pl.BlockSpec(memory_space=VMEM)
    away = pl.BlockSpec(memory_space=pl.ANY)
    return pl.pallas_call(
        forward_kernel,
        out_shape=(
            shape((2, 32, 2048), BF),
            shape((2, 256, 256), BF),
            shape((2, 2, 4, 256, 128), BF),
            shape((2, 256, 1024), BF),
            shape((2, 256, 512), F32),
            shape((2, 256, 512), F32),
            shape((2, 256, 512), BF),
        ),
        in_specs=[here] * 4 + [away] * 5,
        out_specs=(here,) * 7,
        scratch_shapes=[
            VMEM((2, 4, 4, 128, 1408), BF),
            VMEM((2, 4, 4, 688, 128), BF),
            VMEM((2, 1024, 512), BF),
            VMEM((2, 1024, 512), BF),
            VMEM((2, 512, 1024), BF),
            VMEM((2, 2, 4, 256, 128), BF),
            VMEM((256, 2048), BF),
            VMEM((256, 1408), F32),
            VMEM((256, 768), BF),
            VMEM((2, 256, 1024), BF),
            VMEM((2, 2, 4, 256, 128), BF),
            VMEM((2, 4, 256, 128), BF),
            VMEM((2, 4, 256, 128), BF),
            VMEM((2, 4, 256, 128), BF),
            VMEM((2, 2, 4, 256, 256), BF),
            VMEM((2, 4, 256, 256), BF),
            VMEM((2, 4, 256, 256), BF),
            VMEM((2, 4, 256, 256), BF),
            VMEM((2, 2, 4, 256, 256), BF),
            VMEM((8, 32, 256), BF),
            pltpu.SemaphoreType.DMA((N_COPY,)),
            pltpu.SemaphoreType.DMA((N_COPY,)),
            pltpu.SemaphoreType.DMA((N_LOCAL,)),
        ],
        compiler_params=pltpu.CompilerParams(
            collective_id=0, has_side_effects=True, vmem_limit_bytes=67043328
        ),
        name="forward",
    )(tin, tgain, sin, sgain, gu, dn, sg, su, sd)


def total_of_pieces(shard, axis):
    return lax.all_gather(shard, axis).astype(F32).sum(axis=0)


def per_device(
    teacher_in, teacher_gain, t_gate, t_up, t_down,
    student_in, student_gain, s_gate, s_up, s_down, proj, layer_map,
):
    zeros = jnp.zeros((T_LAYERS, 128, 20), BF)
    gu = jnp.concatenate(
        [t_gate[:, :, :640], t_up[:, :, :640], t_gate[:, :, 640:], zeros, t_up[:, :, 640:], zeros], axis=2
    )
    dn = jnp.pad(t_down, ((0, 0), (0, 4), (0, 0)))
    own_states, targets, x_blocks, normeds, gates, ups, units = run_forward(
        teacher_in, teacher_gain, student_in, student_gain, gu, dn, s_gate, s_up, s_down
    )
    joined = [
        jnp.concatenate([x_blocks[l, i % 2, i // 2] for i in range(8)], axis=1) for l in range(S_LAYERS)
    ]
    states = [student_in] + joined
    scales = [None, inverse_rms(states[1].astype(F32))]
    error_parts = []
    deltas = []
    for l in range(S_LAYERS):
        predicted = dot(states[l + 1], proj)
        target = lax.dynamic_index_in_dim(targets, layer_map[l], 0, keepdims=False).astype(F32)
        errors = predicted - target
        error_parts.append(jnp.sum(errors * errors))
        deltas.append((errors * (2.0 / (S_LAYERS * SEQ))).astype(BF))
    error_local = jnp.stack(error_parts)
    grad_x = total_of_pieces(contract_cols(deltas[1], proj).astype(BF), TENSOR)
    gate_grads = [None] * S_LAYERS
    up_grads = [None] * S_LAYERS
    down_grads = [None] * S_LAYERS
    for l in reversed(range(S_LAYERS)):
        grad_out = grad_x.astype(BF)
        grad_units = contract_cols(grad_out, s_down[l])
        sigma = jax.nn.sigmoid(gates[l])
        ga = (grad_units * ups[l] * sigma * (1.0 + gates[l] * (1.0 - sigma))).astype(BF)
        gb = (grad_units * jax.nn.silu(gates[l])).astype(BF)
        gate_grads[l] = contract_rows(normeds[l], ga)
        up_grads[l] = contract_rows(normeds[l], gb)
        down_grads[l] = contract_rows(units[l], grad_out)
        if l > 0:
            norm_part = contract_cols(ga, s_gate[l]) + contract_cols(gb, s_up[l])
            wide = states[l].astype(F32)
            scaled = norm_part * student_gain[l]
            through = scales[l] * scaled - wide * scales[l] ** 3 * jnp.mean(
                wide * scaled, axis=-1, keepdims=True
            )
            part = through + contract_cols(deltas[l - 1], proj)
            grad_x = grad_x + lax.psum(part.astype(BF), TENSOR).astype(F32)
    proj_local = contract_rows(states[1], deltas[0]) + contract_rows(states[2], deltas[1])
    gu_grads = lax.psum_scatter(
        jnp.concatenate(gate_grads + up_grads, axis=1).astype(BF), DP, scatter_dimension=0, tiled=True
    ).astype(F32)
    grad_gate = jnp.stack([gu_grads[:, :512], gu_grads[:, 512:1024]])
    grad_up = jnp.stack([gu_grads[:, 1024:1536], gu_grads[:, 1536:]])
    grad_down = lax.psum_scatter(
        jnp.stack(down_grads).astype(BF), DP, scatter_dimension=2, tiled=True
    ).astype(F32)
    grad_proj = lax.psum_scatter(proj_local.astype(BF), DP, scatter_dimension=0, tiled=True).astype(F32)
    sums = lax.psum(
        jnp.concatenate(
            [
                error_local,
                jnp.stack([jnp.sum(g * g) for g in (grad_gate, grad_up, grad_down, grad_proj)]),
            ]
        ),
        DP_TENSOR,
    )
    counts = jnp.array(
        [S_LAYERS * DS * FS, S_LAYERS * DS * FS, S_LAYERS * DS * FS, DS * DT], F32
    )
    mean_error = sums[:2] / (teacher_in.shape[0] * lax.axis_size(DP) * DT)
    grad_rms = jnp.sqrt(sums[2:] / counts)
    return (own_states, grad_gate, grad_up, grad_down, grad_proj, mean_error, grad_rms)


def solution(mesh):
    finer = Mesh(mesh.devices.reshape(4, 4, 4, 2), ("dp_0", "dp_1", "tensor_0", "tensor_1"))
    placed = (
        P(DP, None),
        P(),
        P(None, DP, TENSOR),
        P(None, DP, TENSOR),
        P(None, TENSOR, DP),
        P(DP, None),
        P(),
        P(None, None, TENSOR),
        P(None, None, TENSOR),
        P(None, TENSOR, None),
        P(None, TENSOR),
        P(),
    )
    return jax.shard_map(
        per_device,
        mesh=finer,
        in_specs=placed,
        out_specs=(
            P(None, DP_TENSOR, None),
            P(None, DP, TENSOR),
            P(None, DP, TENSOR),
            P(None, TENSOR, DP),
            P(DP, TENSOR),
            P(),
            P(),
        ),
        check_vma=False,
    )
```

time: 664 us -> 533 us (0.80)
  waiting for transfers between devices: 459 us -> 243 us
  Pallas kernels: 0 us -> 134 us
  matrix products: 40.5 us -> 16.6 us
  starting transfers between devices: 20 us -> 0.39 us
  other arithmetic: 32.4 us -> 13.3 us
  local copies, waits for them, and re-layouts: 23.4 us -> 38 us
    pallas_call x0 -> x1, Pallas kernels: none -> 134 us  [run_forward(): pl.pallas_call(forward_kernel, out_shape=(shape((2, 32, 2048), BF), shape...]
    all_gather x5 -> x1, waiting for transfers between devices: 151 us -> 26.4 us  [total_of_pieces(): return lax.all_gather(shard, axis).astype(F32).sum(axis=0)]
    unnamed x12 -> x7, waiting for transfers between devices: 82.1 us -> 161 us
    reduce_scatter x2 -> x1, waiting for transfers between devices: 78.1 us -> 0.03 us  [per_device(): lax.psum_scatter(proj_local.astype(BF), DP, scatter_dimension=0, tiled=True)]
    psum x3 -> x1, waiting for transfers between devices: 106 us -> 55 us  [per_device(): grad_x = grad_x + lax.psum(part.astype(BF), TENSOR).astype(F32)]
    all_to_all x4 -> x0, waiting for transfers between devices: 42 us -> none  [the longest x2 25 us: sum_at_owner(): lax.all_to_all(in_blocks(shard, dim, count), axis, 0, 0, tiled=True)]
    all_gather x2 -> x0, blocking collectives: 33 us -> none  [gather_axes(): shard = lax.all_gather(shard, axis, axis=dim, tiled=True)]
    psum x4 -> x1, blocking collectives: 33.9 us -> 66.1 us  [per_device(): lax.psum(jnp.concatenate([error_local, jnp.stack([jnp.sum(g * g) for g in...]
  transfers between devices with their start and end apart: 15 -> 5, of which waited for: 13 -> 4; matrix products, arithmetic and copies ran while one was open for 10% -> 6% of each run, Pallas kernels for 0% -> 0%
where the time goes in v1:
time: 533 us; the launch traced here: 532 us
  waiting for transfers between devices  243 us (46%)
  Pallas kernels  134 us (25%)
  blocking collectives  66.1 us (12%)
  local copies, waits for them, and re-layouts  38 us (7%)
  between operations  20.7 us (4%)
  matrix products  16.6 us (3%)
  other arithmetic  13.3 us (2%)
    unnamed x7, waiting for transfers between devices  161 us
    pallas_call x1, Pallas kernels, run_forward(): pl.pallas_call(forward_kernel, out_shape=(shape((2, 32, 2048), BF), shape...  134 us
    psum x1, blocking collectives, per_device(): lax.psum(jnp.concatenate([error_local, jnp.stack([jnp.sum(g * g) for g in...  66.1 us
    psum x1, waiting for transfers between devices, per_device(): grad_x = grad_x + lax.psum(part.astype(BF), TENSOR).astype(F32)  55 us
    all_gather x1, waiting for transfers between devices, total_of_pieces(): return lax.all_gather(shard, axis).astype(F32).sum(axis=0)  26.4 us
    unnamed x69, local copies, waits for them, and re-layouts  23 us
  transfers between devices with their start and end apart: 5, of which 4 were waited for; matrix products, arithmetic and copies ran while one was open for 6% of the time, Pallas kernels for 0%

profile of v1, /device:TPU:1, one launch (start us, length us, event | category | flops | bytes accessed | tf_op | source)
XLA Modules:
  0.0 532.3 jit_solution(8247549197026551006)
XLA Ops:
  8.1 0.8 slice.131
  8.9 1.2 slice.129
  10.1 0.8 slice.132
  10.8 1.3 fusion.63
  13.5 0.1 copy.42
  13.6 0.1 copy.41
  13.7 0.9 copy.39
  14.6 0.9 copy.40
  15.6 0.8 pad.4.dn_in
  16.4 1.1 concatenate.16.gu_in
  17.5 134.2 %forward.1 = (bf16[2,32,2048]{2,1,0:T(8,128)(2,1)}, bf16[2,256,256]{2,1,0:T(8,128)(2,1)}, bf16[2,2,4,256,128]{4,3,2,1,0:T(8,128)(2,1)}, bf16[2,256,1024]{2,1,0:T...) custom-call(bf16[256,2048]{1,0:T(8,128)(2,1)} %tin.1, ...), custom_call_target="tpu_custom_call" | custom-call | tf_op jit(solution)/shard_map/forward/pallas_call | solution.py:419
  151.8 1.0 bitcast_dynamic-update-slice_fusion.7
  153.5 0.9 bitcast_dynamic-update-slice_fusion.6
  154.4 0.9 bitcast_dynamic-update-slice_fusion.5
  155.3 0.9 bitcast_dynamic-update-slice_fusion.4
  156.2 0.9 bitcast_dynamic-update-slice_fusion.3
  157.1 0.9 bitcast_dynamic-update-slice_fusion.2
  158.1 0.9 bitcast_dynamic-update-slice_fusion.1
  159.0 0.9 bitcast_dynamic-update-slice_fusion
  159.9 0.9 multiply_reduce_fusion.3
  160.8 1.2 convolution_convert_fusion.6
  164.0 0.9 multiply_reduce_fusion.4
  165.0 0.3 fusion.56
  165.3 26.4 %all-gather.3.cloned.1.call-done = bf16[2048,1024]{1,0:T(8,128)(2,1)} async-done(((bf16[256,1024]{1,0:T(8,128)(2,1)}), bf16[2048,1024]{1,0:T(8,128)(2,1)}) %all-gather.3.cloned.1.call-update) | async-done | bytes 4194320 | tf_op jit(solution)/shard_map/all_gather | solution.py:465
  191.7 3.3 convert_reduce_fusion
  195.1 0.6 fusion.36
  195.8 1.0 copy-done.3
  196.8 0.5 fusion.12
  197.3 0.4 copy-done.4
  197.7 0.6 fusion.5
  198.4 1.2 fusion.3
  199.7 2.3 fusion.4
  202.0 0.2 all-reduce.7.cloned.1.call-start
  202.2 1.4 fusion.1
  203.7 55.0 %all-reduce.5.cloned.1.call-done = bf16[256,1024]{1,0:T(8,128)(2,1)} async-done(((bf16[256,1024]{1,0:T(8,128)(2,1)}), bf16[256,1024]{1,0:T(8,128)(2,1)}) %all-reduce.5.cloned.1.call-update) | async-done | bytes 524304 | tf_op jit(solution)/shard_map/psum | solution.py:515
  258.7 1.6 fusion
  260.3 0.2 pad_maximum_fusion.1
  260.5 4.0 copy.33
  264.6 1.7 convolution_convert_fusion.4
  266.4 1.7 convolution_convert_fusion.2
  268.1 0.5 fusion.9
  268.6 0.5 convolution_convert_fusion.3
  269.1 0.7 copy-done.22
  269.8 0.6 convolution_convert_fusion.5
  270.4 2.3 pad_maximum_fusion
  272.7 6.5 %copy.37 = bf16[1024,2048]{1,0:T(8,128)(2,1)} copy(bf16[1024,2048]{0,1:T(8,128)(2,1)} %pad_maximum_fusion) | data formatting | bytes 8388608
  279.3 0.6 copy-done.24
  279.9 0.6 dynamic-slice
  281.2 2.1 multiply_reduce_fusion.5
  283.2 84.1 %all-reduce.7.cloned.1.call-done = bf16[2,512,1024]{1,0,2:T(2,128)(2,1)} async-done(((bf16[2,512,1024]{1,0,2:T(2,128)(2,1)}), bf16[2,512,1024]{1,0,2:T(2,128)(2,1)}) %all-reduce.7.cloned.1.call-update) | async-done | bytes 2097168
  367.4 1.0 dynamic-slice_convert_fusion
  368.4 0.8 copy.36
  369.1 1.8 multiply_reduce_fusion.2
  370.9 77.3 %reduce-scatter.7.cloned.1.call-done = bf16[64,2048]{1,0:T(8,128)(2,1)} async-done(((bf16[1024,2048]{1,0:T(8,128)(2,1)}), bf16[64,2048]{1,0:T(8,128)(2,1)}) %reduce-scatter.7.cloned.1.call-update) | async-done | bytes 262160
  448.2 1.2 copy.38
  449.6 0.7 multiply_reduce_fusion
  450.3 0.9 copy.35
  451.2 0.7 multiply_reduce_fusion.1
  452.0 3.9 concatenate.20
  455.9 0.9 copy.34
  456.8 66.1 %psum.15 = f32[6]{0:T(128)S(1)} all-reduce(f32[6]{0:T(128)S(1)} %concatenate.20), channel_id=1, replica_groups=mesh['dp_0'=4,'dp_1'=4,'tensor_0'=4,'tensor_1'=2] {'dp_0','dp_1','tensor..., use_global_device_ids=true, to_apply=%region_13.14 | all-reduce | flops 6 | bytes 48 | tf_op jit(solution)/shard_map/psum | solution.py:526
  522.9 0.5 slice_multiply_fusion
  523.4 0.6 multiply_sqrt_fusion
  524.0 0.7 copy.60
  (64 shorter events, 0.7 us)
Async XLA Ops:
  8.0 6.6 %slice-start = ((bf16[2,128,684]{1,0,2:T(2,128)(2,1)}), bf16[2,128,640]{1,0,2:T(2,128)(2,1)S(1)}, s32[]{:S(2)}) async-start(bf16[2,128,684]{1,0,2:T(2,128)(2,1)} %param.16), calls=%async_computation.7 | async-start | bytes 655360 | tf_op jit(solution)/shard_map/slice | solution.py:474
  8.0 7.5 %copy-start.15 = (bf16[2,684,128]{2,0,1:T(2,128)(2,1)S(1)}, bf16[2,684,128]{2,0,1:T(2,128)(2,1)}, u32[]{:S(2)}) copy-start(bf16[2,684,128]{2,0,1:T(2,128)(2,1)} %param.17) | copy-start | bytes 1050628
  8.0 183.7 %all-gather.3.cloned.1.call-start = ((), (), s32[]{:S(2)}) async-start(), calls=%async_computation.4 | async-start | bytes 4718592 | tf_op jit(solution)/shard_map/all_gather | solution.py:465
  151.8 8.1 %copy-start = (bf16[1024,256]{1,0:T(8,128)(2,1)S(1)}, bf16[1024,256]{1,0:T(8,128)(2,1)}, u32[]{:S(2)}) copy-start(bf16[1024,256]{1,0:T(8,128)(2,1)} %param.23) | copy-start | bytes 1572868
  151.8 8.1 %copy-start.16 = (bf16[2,256,256]{2,1,0:T(8,128)(2,1)S(1)}, bf16[2,256,256]{2,1,0:T(8,128)(2,1)}, u32[]{:S(2)}) copy-start(bf16[2,256,256]{2,1,0:T(8,128)(2,1)} %get-tuple-element.17) | copy-start | bytes 786436
  157.1 6.3 %copy-start.18 = (f32[2,1024]{1,0:T(2,128)S(1)}, f32[2,1024]{1,0:T(2,128)}, u32[]{:S(2)}) copy-start(f32[2,1024]{1,0:T(2,128)} %sgain.1) | copy-start | bytes 24580
  159.9 31.8 %copy-start.6 = (bf16[256,1024]{1,0:T(8,128)(2,1)}, bf16[256,1024]{1,0:T(8,128)(2,1)S(1)}, u32[]{:S(2)}) copy-start(bf16[256,1024]{1,0:T(8,128)(2,1)S(1)} %get-tuple-element.46) | copy-start | bytes 1572868
  162.0 96.6 %all-reduce.5.cloned.1.call-start = ((), (), s32[]{:S(2)}) async-start(), calls=%async_computation.2 | async-start | bytes 1048576 | tf_op jit(solution)/shard_map/psum | solution.py:515
  165.0 26.8 %copy-start.7 = (f32[256,256]{1,0:T(8,128)}, f32[256,256]{1,0:T(8,128)S(1)}, u32[]{:S(2)}) copy-start(f32[256,256]{1,0:T(8,128)S(1)} %get-tuple-element.71) | copy-start | bytes 786436
  191.7 3.3 copy-start.1
  191.7 3.4 copy-start.19
  191.7 3.4 copy-start.21
  195.1 1.7 copy-start.3
  195.7 2.6 copy-start.11
  195.7 2.6 copy-start.13
  195.8 1.9 copy-start.4
  197.3 1.1 copy-start.8
  199.6 2.6 copy-start.14
  199.6 81.5 %reduce-scatter.5.cloned.1.call-start = ((), (), s32[]{:S(2)}) async-start(), calls=%async_computation.3 | async-start | bytes 557056 | tf_op jit(solution)/shard_map/reduce_scatter | solution.py:525
  202.0 165.4 %all-reduce.7.cloned.1.call-start = ((), (), s32[]{:S(2)}) async-start(), calls=%async_computation.6 | async-start | bytes 4194304
  258.7 1.6 copy-start.5
  264.5 1.8 copy-start.12
  264.5 3.5 copy-start.2
  264.5 183.6 %reduce-scatter.7.cloned.1.call-start = ((), (), s32[]{:S(2)}) async-start(), calls=%async_computation.5 | async-start | bytes 4456448
  264.6 3.5 copy-start.9
  266.4 2.2 copy-start.10
  266.4 2.2 copy-start.20
  268.6 1.2 copy-start.22
  279.3 0.7 copy-start.24
  449.6 73.8 %copy-start.23 = (f32[4]{0:T(128)S(1)}, f32[4]{0:T(128)}, u32[]{:S(2)}) copy-start(f32[4]{0:T(128)} %constant.38) | copy-start | bytes 52
  449.6 74.4 %copy-start.17 = (bf16[2,32,2048]{2,1,0:T(8,128)(2,1)S(1)}, bf16[2,32,2048]{2,1,0:T(8,128)(2,1)}, u32[]{:S(2)}) copy-start(bf16[2,32,2048]{2,1,0:T(8,128)(2,1)} %get-tuple-element.82) | copy-start | bytes 786436
Sparse Core Ops, SparseCore 0:
  162.2 29.5 all-gather.2
  199.7 58.8 all-reduce.4
Sparse Core Ops, SparseCore 1:
  203.3 70.8 reduce-scatter.4
  277.4 90.0 all-reduce.6
  370.6 77.5 reduce-scatter.6

commit v2 on v1

--- a/solution.py
+++ b/solution.py
@@ -21,9 +21,10 @@
 MESH = pl.DeviceIdType.MESH
 BF = jnp.bfloat16
 F32 = jnp.float32
-N_COPY = 104
-N_LOCAL = 9
+N_COPY = 164
+N_LOCAL = 8
 GU_HALVES = ((0, 32, 64), (64, 96, 128))
+WIDTH = (768, 896)
 DN_HALVES = ((0, 176, 352), (352, 512, 688))
 VMEM = pltpu.VMEM
 
@@ -78,6 +79,11 @@
         self.made.append(copy)
         return copy
 
+    def sent(self, some):
+        for copy in some:
+            copy.wait_send()
+        self.made = [copy for copy in self.made if all(copy is not done for done in some)]
+
     def finish(self):
         for copy in self.made:
             copy.wait_send()
@@ -161,6 +167,9 @@
             for copy in pair:
                 copy.wait_recv()
 
+    def sent(self):
+        self.c.sent([copy for pair in self.own + self.fwd + self.row + self.last for copy in pair])
+
 
 class TensorSum:
     def __init__(self, copies, part, pair, both, ring, z, c):
@@ -213,22 +222,109 @@
         self.x.wait_recv()
 
 
+class ScatterSum:
+    def __init__(self, copies, buf, width, got, y, x):
+        self.c, self.buf, self.width, self.got, self.y, self.x = copies, buf, width, got, y, x
+
+    def axes(self, half):
+        if half == 0:
+            return "dp_0", self.y, "dp_1", self.x
+        return "dp_1", self.x, "dp_0", self.y
+
+    def slab(self, half, outer, inner, lo=0, hi=64):
+        r, w = pl.ds(64 * half + lo, hi - lo), pl.ds(0, self.width)
+        return self.buf.at[outer, inner, r, w] if half == 0 else self.buf.at[inner, outer, r, w]
+
+    def one(self):
+        r1 = self.got[0]
+        self.s1 = []
+        for half in (0, 1):
+            b, pb, _, _ = self.axes(half)
+            far = lax.rem(pb + 2, 4)
+            for way, at, k in ((0, 0, 1), (1, 2, 3)):
+                src = self.slab(half, far, pl.ds(at, 2))
+                self.s1.append(
+                    self.c.start(self.c.tags(1)[0], src, r1.at[half, way], {b: lax.rem(pb + k, 4)})
+                )
+
+    def two(self):
+        r1, r2 = self.got[0], self.got[1]
+        self.s2 = []
+        for half in (0, 1):
+            b, pb, _, _ = self.axes(half)
+            for way, at, k in ((0, 0, 1), (1, 2, 3)):
+                to = lax.rem(pb + k, 4)
+                self.s1[2 * half + way].wait_recv()
+                for i in (0, 1):
+                    mine = self.slab(half, to, at + i)
+                    mine[...] = (mine[...].astype(F32) + r1[half, way, i].astype(F32)).astype(BF)
+                src = self.slab(half, to, pl.ds(0, 4))
+                self.s2.append(self.c.start(self.c.tags(1)[0], src, r2.at[half, way], {b: to}))
+
+    def three(self):
+        r2, r3 = self.got[1], self.got[2]
+        self.s3 = []
+        for half in (0, 1):
+            _, pb, a, pa = self.axes(half)
+            self.s2[2 * half].wait_recv()
+            self.s2[2 * half + 1].wait_recv()
+
+            def add(i, carry):
+                k = lax.rem(pa + 2 + i, 4)
+                mine = self.slab(half, pb, k)
+                both = r2[half, 0, k].astype(F32) + r2[half, 1, k].astype(F32)
+                mine[...] = (mine[...].astype(F32) + both).astype(BF)
+                return carry
+
+            add(0, 0)
+            far = lax.rem(pa + 2, 4)
+            for way, lo, k in ((0, 0, 1), (1, 32, 3)):
+                src = self.slab(half, pb, far, lo, lo + 32)
+                self.s3.append(
+                    self.c.start(self.c.tags(1)[0], src, r3.at[half, way], {a: lax.rem(pa + k, 4)})
+                )
+            lax.fori_loop(1, 4, add, 0)
+
+    def four(self):
+        r3, r4 = self.got[2], self.got[3]
+        self.s4 = []
+        for half in (0, 1):
+            _, pb, a, pa = self.axes(half)
+            for way, lo, k in ((0, 0, 1), (1, 32, 3)):
+                to = lax.rem(pa + k, 4)
+                self.s3[2 * half + way].wait_recv()
+                mine = self.slab(half, pb, to, lo, lo + 32)
+                mine[...] = (mine[...].astype(F32) + r3[half, way].astype(F32)).astype(BF)
+                src = self.slab(half, pb, to)
+                self.s4.append(self.c.start(self.c.tags(1)[0], src, r4.at[half, way], {a: to}))
+
+    def five(self, half):
+        r4 = self.got[3]
+        _, pb, _, pa = self.axes(half)
+        self.s4[2 * half].wait_recv()
+        self.s4[2 * half + 1].wait_recv()
+        mine = self.slab(half, pb, pa)
+        return mine[...].astype(F32) + r4[half, 0].astype(F32) + r4[half, 1].astype(F32)
+
+
 def blocks(ref, *lead, rows=slice(None)):
     return jnp.concatenate([ref[lead + (t % 2, t // 2, rows)] for t in range(8)], axis=1)
 
 
-def forward_kernel(
-    tin, tgain, sin, sgain, gu_in, dn_in, sg_in, su_in, sd_in,
-    states_out, target_out, x_out, sn_out, a_out, b_out, u_out,
-    wg, wd, sg, su, sd, xs, tn, acts, hid, sn,
+def step_kernel(
+    lmap, tin, tgain, sin, sgain, gu_in, dn_in, sg_in, su_in, sd_in, proj_in,
+    states_out, gate_out, up_out, down_out, proj_out, mean_out,
+    wg, wd, sg, su, sd, proj, xs, tn, acts, hid, sn, snt, a_out, b_out, u_out,
     spart, spair, sboth, sring, tpart, tpair, tboth, tring, hn, rows_in,
+    pred, delta, gpart, gpair, gboth, gring, gnew, gwide, gyt, ga, gb, side,
+    r11, r12, r13, r14, r01, r02, r03, r04, stat, stat_y, stat_x, stat_t,
     send, recv, local,
 ):
     y, x = lax.axis_index("dp_0"), lax.axis_index("dp_1")
     z, c = lax.axis_index("tensor_0"), lax.axis_index("tensor_1")
     t = 2 * z + c
-    peers = [{"dp_0": lax.rem(y + k, 4)} for k in (1, 3)]
-    peers += [{"dp_1": lax.rem(x + k, 4)} for k in (1, 3)]
+    peers = [{"dp_0": lax.rem(y + k, 4)} for k in (1, 2, 3)]
+    peers += [{"dp_1": lax.rem(x + k, 4)} for k in (1, 2, 3)]
     others = [lax.rem(t + k, 8) for k in range(1, 8)]
     peers += [{"tensor_0": o // 2, "tensor_1": lax.rem(o, 2)} for o in others]
     barrier = pltpu.get_barrier_semaphore()
@@ -249,6 +345,7 @@
     load(sg_in, sg)
     load(su_in, su)
     load(sd_in, sd)
+    load(proj_in, proj)
     gu = [Gather(copies, wg.at[l], GU_HALVES, y, x) for l in (0, 1)]
     dn = [Gather(copies, wd.at[l], DN_HALVES, y, x) for l in (0, 1)]
     pl.semaphore_wait(barrier, len(peers))
@@ -338,12 +435,15 @@
             old = hn[0, c, z]
         new = (old.astype(F32) + tsum[k].total()).astype(BF)
         hn[k, c, z] = new
-        target_out[k] = new
+
+    def predict(l):
+        pred[l] = dot(blocks(xs, l), proj[...])
+        snt[l] = sn[l].T
 
     def student(l):
         student_norm(l)
         if l == 0:
-            for copy in loads[4:7]:
+            for copy in loads[4:8]:
                 copy.wait()
         student_units(l)
         student_part(l)
@@ -355,6 +455,124 @@
         sgather[l].along()
         sgather[l].across()
         sgather[l].complete()
+
+    gsum = [TensorSum(copies, gpart.at[l], gpair.at[l], gboth.at[l], gring.at[l], z, c) for l in (0, 1)]
+    ggather = [TensorGather(copies, gnew.at[l], z, c) for l in (0, 1)]
+    scatter = {
+        1: ScatterSum(copies, wg.at[0], 896, (r11, r12, r13, r14), y, x),
+        0: ScatterSum(copies, wg.at[1], 768, (r01, r02, r03, r04), y, x),
+    }
+
+    def error(l):
+        target = jnp.where(lmap[l] == 0, hn[0, c, z].astype(F32), hn[1, c, z].astype(F32))
+        e = pred[l] - target
+        delta[l] = (e * (2.0 / (S_LAYERS * SEQ))).astype(BF)
+        return jnp.sum(jnp.sum(e * e, axis=1, keepdims=True), axis=0, keepdims=True)
+
+    def top_part():
+        def body(i, carry):
+            p = contract_cols(delta[1], proj[pl.ds(pl.multiple_of(i * 256, 256), 256), :])
+            gpart[1, 0, i] = p[:, :128].astype(BF)
+            gpart[1, 1, i] = p[:, 128:].astype(BF)
+            return carry
+
+        lax.fori_loop(0, 4, body, 0)
+
+    def side_part():
+        def body(n):
+            side[:, pl.ds(n, 256)] = contract_cols(delta[0], proj[pl.ds(n, 256), :])
+
+        loop(1024, 256, body)
+
+    def cuts(l, at, width, half):
+        lo, hi = max(at, half * WIDTH[l]), min(at + width, (half + 1) * WIDTH[l])
+        return [(lo, hi)] if lo < hi else []
+
+    def put(l, at, g):
+        for half in (0, 1):
+            for lo, hi in cuts(l, at, g.shape[1], half):
+                v = g[:, lo - at:hi - at].reshape(4, 4, 64, hi - lo).astype(BF)
+                wg[1 - l, :, :, 64 * half:64 * half + 64, lo - half * WIDTH[l]:hi - half * WIDTH[l]] = v
+
+    def proj_grad():
+        g = contract_rows(blocks(xs, 0), delta[0]) + contract_rows(blocks(xs, 1), delta[1])
+        put(1, 1536, g)
+
+    def units_back(l):
+        sn[l] = blocks(gnew, l)
+
+        def body(n):
+            cols = pl.ds(n, 256)
+            du = contract_cols(sn[l], sd[l, cols, :])
+            a, b = a_out[l, :, cols], b_out[l, :, cols]
+            s = 1.0 / (1.0 + jnp.exp(-a))
+            ga[l, :, cols] = (du * b * s * (1.0 + a * (1.0 - s))).astype(BF)
+            gb[l, :, cols] = (du * (a * s)).astype(BF)
+
+        loop(512, 256, body)
+
+    def norm_part():
+        def body(n):
+            rows = pl.ds(n, 256)
+            acts[:, rows] = contract_cols(ga[1], sg[1, rows, :]) + contract_cols(gb[1], su[1, rows, :])
+
+        loop(1024, 256, body)
+
+        def through(r):
+            rows = pl.ds(r, 32)
+            v = blocks(xs, 0, rows=rows).astype(F32)
+            scale = inverse_rms(v)
+            q = acts[rows, 0:1024] * sgain[1:2, :]
+            m = jnp.mean(v * q, axis=-1, keepdims=True)
+            p = scale * q - v * (scale * scale * scale) * m + side[rows, :]
+            for i in range(8):
+                gpart[0, i % 2, i // 2, rows, :] = p[:, i * 128:(i + 1) * 128].astype(BF)
+
+        loop(256, 32, through)
+
+    def weight_grads(l):
+        gyt[...] = sn[l].T
+        for at, left, right in ((0, snt.at[l], ga), (512, snt.at[l], gb), (1024, gyt, u_out)):
+            for n in (0, 256):
+                put(l, at + n, dot(left[...], right[l, :, n:n + 256]))
+
+    def grads_end(l):
+        found = {}
+        for half in (0, 1):
+            g = scatter[l].five(half)
+            for out, lo, hi in ((gate_out, 0, 512), (up_out, 512, 1024), (down_out, 1024, 1536), (proj_out, 1536, 1792)):
+                for b, e in cuts(l, lo, hi - lo, half):
+                    v = g[:, b - half * WIDTH[l]:e - half * WIDTH[l]]
+                    if out is proj_out:
+                        out[:, b - lo:e - lo] = v
+                    else:
+                        out[l, :, b - lo:e - lo] = v
+                    v = jnp.sum(jnp.sum(v * v, axis=1, keepdims=True), axis=0, keepdims=True)
+                    found[lo] = found[lo] + v if lo in found else v
+        return [found[lo] for lo in sorted(found)]
+
+    def totals(values):
+        for i, v in enumerate(values):
+            stat[0, i:i + 1, :] = jnp.broadcast_to(v, (1, 128))
+        stat[0, 6:8, :] = jnp.zeros((2, 128), F32)
+        steps = (
+            (stat_y, y, [(lax.rem(y + k, 4), {"dp_0": lax.rem(y + k, 4)}) for k in (2, 1, 3)]),
+            (stat_x, x, [(lax.rem(x + k, 4), {"dp_1": lax.rem(x + k, 4)}) for k in (2, 1, 3)]),
+            (stat_t, t, [(o, {"tensor_0": o // 2, "tensor_1": lax.rem(o, 2)}) for o in others]),
+        )
+        for i, (got, me, targets) in enumerate(steps):
+            sent = [
+                copies.start(copies.tags(1)[0], stat.at[i], got.at[me], where) for _, where in targets
+            ]
+            acc = stat[i]
+            got[me] = acc
+            for copy in sent:
+                copy.wait_recv()
+            total = got[0]
+            for k in range(1, got.shape[0]):
+                total = total + got[k]
+            stat[i + 1] = total
+        return total
 
     teacher_norm(0)
     gu[0].first_forward()
@@ -387,8 +605,8 @@
     tgather.complete()
     teacher_norm(1)
     gu[1].second_forward()
-    x_out[...] = xs[...]
-    sn_out[...] = sn[...]
+    predict(0)
+    predict(1)
     for i in range(8):
         states_out[0, :, i * 256:(i + 1) * 256] = hn[0, i % 2, i // 2, pl.ds(pl.multiple_of(t * 32, 32), 32), :]
     dn[1].second_forward()
@@ -399,47 +617,92 @@
     tsum[1].across()
     tsum[1].along()
     teacher_result(1)
+    e1 = error(1)
+    top_part()
+    gsum[1].across()
+    e0 = error(0)
+    side_part()
+    gsum[1].along()
     shared = []
     for o in others:
         rows = pl.ds(pl.multiple_of(o * 32, 32), 32)
         where = {"tensor_0": o // 2, "tensor_1": lax.rem(o, 2)}
         shared.append(copies.start(copies.tags(1)[0], hn.at[1, c, z, rows], rows_in.at[t], where))
     rows_in[t] = hn[1, c, z, pl.ds(pl.multiple_of(t * 32, 32), 32), :]
+    gu[0].sent()
+    proj_grad()
+    gwide[...] = gsum[1].total()
+    gnew[1, c, z] = gwide[...].astype(BF)
+    ggather[1].along()
+    ggather[1].across()
+    ggather[1].complete()
+    units_back(1)
+    norm_part()
+    gsum[0].across()
+    weight_grads(1)
+    scatter[1].one()
+    gsum[0].along()
+    scatter[1].two()
+    gwide[...] = gwide[...] + gsum[0].total()
+    gnew[0, c, z] = gwide[...].astype(BF)
+    ggather[0].along()
+    ggather[0].across()
+    ggather[0].complete()
+    units_back(0)
+    gu[1].sent()
+    weight_grads(0)
+    scatter[0].one()
+    scatter[1].three()
+    scatter[0].two()
+    scatter[1].four()
+    scatter[0].three()
+    found = grads_end(1)
+    scatter[0].four()
     for copy in shared:
         copy.wait_recv()
     for i in range(8):
         states_out[1, :, i * 256:(i + 1) * 256] = rows_in[i]
+    more = grads_end(0)
+    found = [found[i] + more[i] for i in range(3)] + found[3:]
+    total = totals([e0, e1] + found)
+    mean_out[0:2, :] = total[0:2] / float(4096 * DT)
+    mean_out[2:5, :] = jnp.sqrt(total[2:5] / float(S_LAYERS * DS * FS))
+    mean_out[5:8, :] = jnp.sqrt(total[5:8] / float(DS * DT))
     copies.finish()
 
 
-def run_forward(tin, tgain, sin, sgain, gu, dn, sg, su, sd):
+def run(lmap, tin, tgain, sin, sgain, gu, dn, sg, su, sd, proj):
     shape = jax.ShapeDtypeStruct
     here = pl.BlockSpec(memory_space=VMEM)
     away = pl.BlockSpec(memory_space=pl.ANY)
     return pl.pallas_call(
-        forward_kernel,
+        step_kernel,
         out_shape=(
             shape((2, 32, 2048), BF),
-            shape((2, 256, 256), BF),
-            shape((2, 2, 4, 256, 128), BF),
-            shape((2, 256, 1024), BF),
-            shape((2, 256, 512), F32),
-            shape((2, 256, 512), F32),
-            shape((2, 256, 512), BF),
+            shape((2, 64, 512), F32),
+            shape((2, 64, 512), F32),
+            shape((2, 64, 512), F32),
+            shape((64, 256), F32),
+            shape((8, 128), F32),
         ),
-        in_specs=[here] * 4 + [away] * 5,
-        out_specs=(here,) * 7,
+        in_specs=[pl.BlockSpec(memory_space=pltpu.SMEM)] + [here] * 4 + [away] * 6,
+        out_specs=(here,) * 6,
         scratch_shapes=[
             VMEM((2, 4, 4, 128, 1408), BF),
             VMEM((2, 4, 4, 688, 128), BF),
             VMEM((2, 1024, 512), BF),
             VMEM((2, 1024, 512), BF),
             VMEM((2, 512, 1024), BF),
+            VMEM((1024, 256), BF),
             VMEM((2, 2, 4, 256, 128), BF),
             VMEM((256, 2048), BF),
             VMEM((256, 1408), F32),
             VMEM((256, 768), BF),
             VMEM((2, 256, 1024), BF),
+            VMEM((2, 1024, 256), BF),
+            VMEM((2, 256, 512), F32),
+            VMEM((2, 256, 512), F32),
+            VMEM((2, 256, 512), BF),
             VMEM((2, 2, 4, 256, 128), BF),
             VMEM((2, 4, 256, 128), BF),
             VMEM((2, 4, 256, 128), BF),
@@ -450,6 +713,29 @@
             VMEM((2, 4, 256, 256), BF),
             VMEM((2, 2, 4, 256, 256), BF),
             VMEM((8, 32, 256), BF),
+            VMEM((2, 256, 256), F32),
+            VMEM((2, 256, 256), BF),
+            VMEM((2, 2, 4, 256, 128), BF),
+            VMEM((2, 4, 256, 128), BF),
+            VMEM((2, 4, 256, 128), BF),
+            VMEM((2, 4, 256, 128), BF),
+            VMEM((2, 2, 4, 256, 128), BF),
+            VMEM((256, 128), F32),
+            VMEM((1024, 256), BF),
+            VMEM((2, 256, 512), BF),
+            VMEM((2, 256, 512), BF),
+            VMEM((256, 1024), F32),
+        ]
+        + [
+            VMEM(s, BF)
+            for w in (896, 768)
+            for s in ((2, 2, 2, 64, w), (2, 2, 4, 64, w), (2, 2, 32, w), (2, 2, 64, w))
+        ]
+        + [
+            VMEM((4, 8, 128), F32),
+            VMEM((4, 8, 128), F32),
+            VMEM((4, 8, 128), F32),
+            VMEM((8, 8, 128), F32),
             pltpu.SemaphoreType.DMA((N_COPY,)),
             pltpu.SemaphoreType.DMA((N_COPY,)),
             pltpu.SemaphoreType.DMA((N_LOCAL,)),
@@ -457,12 +743,8 @@
         compiler_params=pltpu.CompilerParams(
             collective_id=0, has_side_effects=True, vmem_limit_bytes=67043328
         ),
-        name="forward",
-    )(tin, tgain, sin, sgain, gu, dn, sg, su, sd)
-
-
-def total_of_pieces(shard, axis):
-    return lax.all_gather(shard, axis).astype(F32).sum(axis=0)
+        name="step",
+    )(lmap, tin, tgain, sin, sgain, gu, dn, sg, su, sd, proj)
 
 
 def per_device(
@@ -474,70 +756,10 @@
         [t_gate[:, :, :640], t_up[:, :, :640], t_gate[:, :, 640:], zeros, t_up[:, :, 640:], zeros], axis=2
     )
     dn = jnp.pad(t_down, ((0, 0), (0, 4), (0, 0)))
-    own_states, targets, x_blocks, normeds, gates, ups, units = run_forward(
-        teacher_in, teacher_gain, student_in, student_gain, gu, dn, s_gate, s_up, s_down
+    own_states, gate, up, down, width, stats = run(
+        layer_map, teacher_in, teacher_gain, student_in, student_gain, gu, dn, s_gate, s_up, s_down, proj
     )
-    joined = [
-        jnp.concatenate([x_blocks[l, i % 2, i // 2] for i in range(8)], axis=1) for l in range(S_LAYERS)
-    ]
-    states = [student_in] + joined
-    scales = [None, inverse_rms(states[1].astype(F32))]
-    error_parts = []
-    deltas = []
-    for l in range(S_LAYERS):
-        predicted = dot(states[l + 1], proj)
-        target = lax.dynamic_index_in_dim(targets, layer_map[l], 0, keepdims=False).astype(F32)
-        errors = predicted - target
-        error_parts.append(jnp.sum(errors * errors))
-        deltas.append((errors * (2.0 / (S_LAYERS * SEQ))).astype(BF))
-    error_local = jnp.stack(error_parts)
-    grad_x = total_of_pieces(contract_cols(deltas[1], proj).astype(BF), TENSOR)
-    gate_grads = [None] * S_LAYERS
-    up_grads = [None] * S_LAYERS
-    down_grads = [None] * S_LAYERS
-    for l in reversed(range(S_LAYERS)):
-        grad_out = grad_x.astype(BF)
-        grad_units = contract_cols(grad_out, s_down[l])
-        sigma = jax.nn.sigmoid(gates[l])
-        ga = (grad_units * ups[l] * sigma * (1.0 + gates[l] * (1.0 - sigma))).astype(BF)
-        gb = (grad_units * jax.nn.silu(gates[l])).astype(BF)
-        gate_grads[l] = contract_rows(normeds[l], ga)
-        up_grads[l] = contract_rows(normeds[l], gb)
-        down_grads[l] = contract_rows(units[l], grad_out)
-        if l > 0:
-            norm_part = contract_cols(ga, s_gate[l]) + contract_cols(gb, s_up[l])
-            wide = states[l].astype(F32)
-            scaled = norm_part * student_gain[l]
-            through = scales[l] * scaled - wide * scales[l] ** 3 * jnp.mean(
-                wide * scaled, axis=-1, keepdims=True
-            )
-            part = through + contract_cols(deltas[l - 1], proj)
-            grad_x = grad_x + lax.psum(part.astype(BF), TENSOR).astype(F32)
-    proj_local = contract_rows(states[1], deltas[0]) + contract_rows(states[2], deltas[1])
-    gu_grads = lax.psum_scatter(
-        jnp.concatenate(gate_grads + up_grads, axis=1).astype(BF), DP, scatter_dimension=0, tiled=True
-    ).astype(F32)
-    grad_gate = jnp.stack([gu_grads[:, :512], gu_grads[:, 512:1024]])
-    grad_up = jnp.stack([gu_grads[:, 1024:1536], gu_grads[:, 1536:]])
-    grad_down = lax.psum_scatter(
-        jnp.stack(down_grads).astype(BF), DP, scatter_dimension=2, tiled=True
-    ).astype(F32)
-    grad_proj = lax.psum_scatter(proj_local.astype(BF), DP, scatter_dimension=0, tiled=True).astype(F32)
-    sums = lax.psum(
-        jnp.concatenate(
-            [
-                error_local,
-                jnp.stack([jnp.sum(g * g) for g in (grad_gate, grad_up, grad_down, grad_proj)]),
-            ]
-        ),
-        DP_TENSOR,
-    )
-    counts = jnp.array(
-        [S_LAYERS * DS * FS, S_LAYERS * DS * FS, S_LAYERS * DS * FS, DS * DT], F32
-    )
-    mean_error = sums[:2] / (teacher_in.shape[0] * lax.axis_size(DP) * DT)
-    grad_rms = jnp.sqrt(sums[2:] / counts)
-    return (own_states, grad_gate, grad_up, grad_down, grad_proj, mean_error, grad_rms)
+    return (own_states, gate, up, jnp.swapaxes(down, 1, 2), width, stats[0:2, 0], stats[2:6, 0])
 
 
 def solution(mesh):

time: 533 us -> 220 us (0.41)
  waiting for transfers between devices: 243 us -> 0 us
  Pallas kernels: 134 us -> 202 us
  blocking collectives: 66.1 us -> 0 us
  local copies, waits for them, and re-layouts: 38 us -> 16.7 us
  between operations: 20.7 us -> 0.71 us
  matrix products: 16.6 us -> 0 us
  other arithmetic: 13.3 us -> 0 us
    unnamed x7 -> x0, waiting for transfers between devices: 161 us -> none
    pallas_call x1, Pallas kernels: 134 us -> 202 us  [run(): pl.pallas_call(step_kernel, out_shape=(shape((2, 32, 2048), BF), shape((2...]
    psum x1 -> x0, blocking collectives: 66.1 us -> none  [per_device(): lax.psum(jnp.concatenate([error_local, jnp.stack([jnp.sum(g * g) for g in...]
    psum x1 -> x0, waiting for transfers between devices: 55 us -> none  [per_device(): grad_x = grad_x + lax.psum(part.astype(BF), TENSOR).astype(F32)]
    all_gather x1 -> x0, waiting for transfers between devices: 26.4 us -> none  [total_of_pieces(): return lax.all_gather(shard, axis).astype(F32).sum(axis=0)]
    dot_general x16 -> x0, matrix products: 16.6 us -> none  [the longest x8 10.2 us: contract_rows(): lax.dot_general(left, right, (((0,), (0,)), ((), ())), preferred_element_...]
    unnamed x69 -> x14, local copies, waits for them, and re-layouts: 23 us -> 9.44 us
    reduce_sum x5 -> x0, other arithmetic: 8.65 us -> none  [the longest x4 5.33 us: per_device(): jnp.sum(g * g)]
  transfers between devices with their start and end apart: 5 -> 0, of which waited for: 4 -> 0; matrix products, arithmetic and copies ran while one was open for 6% -> 0% of each run, Pallas kernels for 0% -> 0%
where the time goes in v2:
time: 220 us
  Pallas kernels  202 us (92%)
  local copies, waits for them, and re-layouts  16.7 us (8%)
    pallas_call x1, Pallas kernels, run(): pl.pallas_call(step_kernel, out_shape=(shape((2, 32, 2048), BF), shape((2...  202 us
    unnamed x14, local copies, waits for them, and re-layouts  9.44 us

profile of v2, /device:TPU:1, one launch (start us, length us, event | category | flops | bytes accessed | tf_op | source)
XLA Modules:
  0.0 220.0 jit_solution(2633619632061056040)
XLA Ops:
  0.6 0.0 slice-start
  0.6 0.8 slice.20
  1.4 0.8 slice.21
  2.2 0.1 copy.32
  2.3 0.1 copy.31
  2.5 0.0 copy-start
  2.5 1.2 slice.18
  3.7 0.9 copy.29
  4.6 0.0 slice-done
  4.7 0.9 copy.30
  5.6 1.1 concatenate.3.gu_in
  6.7 0.0 copy-done
  6.7 0.8 pad.4.dn_in
  7.5 202.5 %step.1 = (bf16[2,32,2048]{2,1,0:T(8,128)(2,1)}, f32[2,64,512]{2,1,0:T(8,128)}, f32[2,64,512]{2,1,0:T(8,128)}, f32[2,64,512]{2,1,0:T(8,128)}, f32[64,256]{1,0:T(8,128)}, /*index=5*/f32[8,128]{1,0:T(8,128)}) custom-call(s32[2]{0:T(128)} %lmap.1, bf16[256,2048]{1,0:T(8,128)(2,1)} %tin.1, f32[2,2048]{1,0:T(2,128)} %tgain.1, bf16[256,1024]{1,0:T(8,128)(2,1)} %sin.1, ...), custom_call_target="tpu_custom_call" | custom-call | tf_op jit(solution)/shard_map/step/pallas_call | solution.py:678
  210.0 0.0 copy-start.1
  210.0 1.3 slice_reduce_fusion
  211.3 1.3 slice_reduce_fusion.1
  212.6 1.7 copy.38
  214.3 1.7 copy.39
  216.0 1.7 copy.40
  217.7 1.7 copy.41
  219.3 0.0 copy-done.1
  219.3 0.6 copy.42
  (2 shorter events, 0.1 us)
Async XLA Ops:
  0.6 4.0 %slice-start = ((bf16[2,128,684]{1,0,2:T(2,128)(2,1)}), bf16[2,128,640]{1,0,2:T(2,128)(2,1)S(1)}, s32[]{:S(2)}) async-start(bf16[2,128,684]{1,0,2:T(2,128)(2,1)} %param.15), calls=%async_computation | async-start | bytes 655360 | tf_op jit(solution)/shard_map/slice | solution.py:756
  2.5 4.2 %copy-start = (bf16[2,684,128]{2,0,1:T(2,128)(2,1)S(1)}, bf16[2,684,128]{2,0,1:T(2,128)(2,1)}, u32[]{:S(2)}) copy-start(bf16[2,684,128]{2,0,1:T(2,128)(2,1)} %param.16) | copy-start | bytes 1050628
  210.0 9.3 %copy-start.1 = (f32[64,256]{1,0:T(8,128)S(1)}, f32[64,256]{1,0:T(8,128)}, u32[]{:S(2)}) copy-start(f32[64,256]{1,0:T(8,128)} %get-tuple-element.30) | copy-start | bytes 196612

commit v3 on v2

--- a/solution.py
+++ b/solution.py
@@ -21,10 +21,18 @@
 MESH = pl.DeviceIdType.MESH
 BF = jnp.bfloat16
 F32 = jnp.float32
-N_COPY = 164
-N_LOCAL = 8
-GU_HALVES = ((0, 32, 64), (64, 96, 128))
-WIDTH = (768, 896)
+N_COPY = 244
+N_LOCAL = 11
+GU_HALVES = ((0, 352, 688), (688, 1040, 1376))
+CHUNKS = (
+    ("d1", 0, 0, 128),
+    ("g1", 0, 256, 128),
+    ("u1", 0, 512, 128),
+    ("p", 0, 768, 64),
+    ("d0", 1, 0, 128),
+    ("g0", 1, 256, 128),
+    ("u0", 1, 512, 128),
+)
 DN_HALVES = ((0, 176, 352), (352, 512, 688))
 VMEM = pltpu.VMEM
 
@@ -223,17 +231,17 @@
 
 
 class ScatterSum:
-    def __init__(self, copies, buf, width, got, y, x):
-        self.c, self.buf, self.width, self.got, self.y, self.x = copies, buf, width, got, y, x
+    def __init__(self, copies, buf, base, rows, got, y, x):
+        self.c, self.buf, self.base, self.rows, self.got, self.y, self.x = copies, buf, base, rows, got, y, x
 
     def axes(self, half):
         if half == 0:
             return "dp_0", self.y, "dp_1", self.x
         return "dp_1", self.x, "dp_0", self.y
 
-    def slab(self, half, outer, inner, lo=0, hi=64):
-        r, w = pl.ds(64 * half + lo, hi - lo), pl.ds(0, self.width)
-        return self.buf.at[outer, inner, r, w] if half == 0 else self.buf.at[inner, outer, r, w]
+    def slab(self, half, outer, inner, lo=0, hi=None):
+        r = pl.ds(self.base + self.rows * half + lo, (self.rows if hi is None else hi) - lo)
+        return self.buf.at[outer, inner, r] if half == 0 else self.buf.at[inner, outer, r]
 
     def one(self):
         r1 = self.got[0]
@@ -278,8 +286,8 @@
 
             add(0, 0)
             far = lax.rem(pa + 2, 4)
-            for way, lo, k in ((0, 0, 1), (1, 32, 3)):
-                src = self.slab(half, pb, far, lo, lo + 32)
+            for way, lo, k in ((0, 0, 1), (1, self.rows // 2, 3)):
+                src = self.slab(half, pb, far, lo, lo + self.rows // 2)
                 self.s3.append(
                     self.c.start(self.c.tags(1)[0], src, r3.at[half, way], {a: lax.rem(pa + k, 4)})
                 )
@@ -290,10 +298,10 @@
         self.s4 = []
         for half in (0, 1):
             _, pb, a, pa = self.axes(half)
-            for way, lo, k in ((0, 0, 1), (1, 32, 3)):
+            for way, lo, k in ((0, 0, 1), (1, self.rows // 2, 3)):
                 to = lax.rem(pa + k, 4)
                 self.s3[2 * half + way].wait_recv()
-                mine = self.slab(half, pb, to, lo, lo + 32)
+                mine = self.slab(half, pb, to, lo, lo + self.rows // 2)
                 mine[...] = (mine[...].astype(F32) + r3[half, way].astype(F32)).astype(BF)
                 src = self.slab(half, pb, to)
                 self.s4.append(self.c.start(self.c.tags(1)[0], src, r4.at[half, way], {a: to}))
@@ -312,14 +320,13 @@
 
 
 def step_kernel(
-    lmap, tin, tgain, sin, sgain, gu_in, dn_in, sg_in, su_in, sd_in, proj_in,
+    lmap, tin, tgain, sin, sgain, gate_in, up_in, dn_in, sg_in, su_in, sd_in, proj_in,
     states_out, gate_out, up_out, down_out, proj_out, mean_out,
     wg, wd, sg, su, sd, proj, xs, tn, acts, hid, sn, snt, a_out, b_out, u_out,
     spart, spair, sboth, sring, tpart, tpair, tboth, tring, hn, rows_in,
-    pred, delta, gpart, gpair, gboth, gring, gnew, gwide, gyt, ga, gb, side,
-    r11, r12, r13, r14, r01, r02, r03, r04, stat, stat_y, stat_x, stat_t,
-    send, recv, local,
+    pred, delta, gpart, gpair, gboth, gring, gnew, gwide, gyt, ga, gb, side, *rest,
 ):
+    sums, (stat, stat_y, stat_x, stat_t, send, recv, local) = rest[:-7], rest[-7:]
     y, x = lax.axis_index("dp_0"), lax.axis_index("dp_1")
     z, c = lax.axis_index("tensor_0"), lax.axis_index("tensor_1")
     t = 2 * z + c
@@ -340,8 +347,13 @@
         loads.append(copy)
 
     for l in (0, 1):
-        load(gu_in.at[l], wg.at[l, y, x])
-        load(dn_in.at[l], wd.at[l, y, x])
+        wg[l, y, x, 684:688, :] = jnp.zeros((4, 128), BF)
+        wg[l, y, x, 1372:1376, :] = jnp.zeros((4, 128), BF)
+        wd[l, y, x, 684:688, :] = jnp.zeros((4, 128), BF)
+    for l in (0, 1):
+        load(gate_in.at[l], wg.at[l, y, x, pl.ds(0, 684)])
+        load(up_in.at[l], wg.at[l, y, x, pl.ds(688, 684)])
+        load(dn_in.at[l], wd.at[l, y, x, pl.ds(0, 684)])
     load(sg_in, sg)
     load(su_in, su)
     load(sd_in, sd)
@@ -350,8 +362,9 @@
     dn = [Gather(copies, wd.at[l], DN_HALVES, y, x) for l in (0, 1)]
     pl.semaphore_wait(barrier, len(peers))
     loads[0].wait()
+    loads[1].wait()
     gu[0].first()
-    loads[1].wait()
+    loads[2].wait()
     dn[0].first()
 
     def teacher_norm(k):
@@ -391,30 +404,23 @@
         lax.fori_loop(0, 4, body, 0)
 
     def teacher_up(k):
-        def body(n):
-            cols = pl.ds(n, 256)
-            w = wg[k, :, :, :, cols].reshape(DT, 256)
-            acts[:, cols] = dot(tn[...], w)
-
-        loop(1280, 256, body)
-        acts[:, 1280:1408] = dot(tn[...], wg[k, :, :, :, 1280:1408].reshape(DT, 128))
-
-        def unit(r):
-            rows = pl.ds(r, 32)
-            hid[rows, 0:640] = (silu(acts[rows, 0:640]) * acts[rows, 640:1280]).astype(BF)
-            tail = acts[rows, 1280:1408]
-            hid[rows, 640:768] = (silu(tail) * pltpu.roll(tail, 64, 1)).astype(BF)
-
-        loop(256, 32, unit)
-
-    def teacher_down(k):
+        for lo, wide in ((0, 256), (256, 256), (512, 176)):
+            both = [
+                contract_cols(
+                    tn[...],
+                    jnp.concatenate([wg[k, p, q, at + lo:at + lo + wide, :] for p in range(4) for q in range(4)], axis=1),
+                )
+                for at in (0, 688)
+            ]
+            hid[:, lo:lo + wide] = (silu(both[0]) * both[1]).astype(BF)
+
+    def teacher_down(k, half):
         def body(i, carry):
-            q = 2 * lax.rem(i, 2)
-            w = jnp.concatenate([wd[k, i // 2, q], wd[k, i // 2, q + 1]], axis=1)
-            tpart[k, lax.rem(i, 2), i // 2] = dot(hid[:, 0:688], w).astype(BF)
+            w = jnp.concatenate([wd[k, i, 2 * half], wd[k, i, 2 * half + 1]], axis=1)
+            tpart[k, half, i] = dot(hid[:, 0:688], w).astype(BF)
             return carry
 
-        lax.fori_loop(0, 8, body, 0)
+        lax.fori_loop(0, 4, body, 0)
 
     ssum = [TensorSum(copies, spart.at[l], spair.at[l], sboth.at[l], sring.at[l], z, c) for l in (0, 1)]
     sgather = [TensorGather(copies, xs.at[l], z, c) for l in (0, 1)]
@@ -443,7 +449,7 @@
     def student(l):
         student_norm(l)
         if l == 0:
-            for copy in loads[4:8]:
+            for copy in loads[6:10]:
                 copy.wait()
         student_units(l)
         student_part(l)
@@ -458,10 +464,9 @@
 
     gsum = [TensorSum(copies, gpart.at[l], gpair.at[l], gboth.at[l], gring.at[l], z, c) for l in (0, 1)]
     ggather = [TensorGather(copies, gnew.at[l], z, c) for l in (0, 1)]
-    scatter = {
-        1: ScatterSum(copies, wg.at[0], 896, (r11, r12, r13, r14), y, x),
-        0: ScatterSum(copies, wg.at[1], 768, (r01, r02, r03, r04), y, x),
-    }
+    scatter = {}
+    for i, (key, k, base, rows) in enumerate(CHUNKS):
+        scatter[key] = ScatterSum(copies, wg.at[k], base, rows, sums[4 * i:4 * i + 4], y, x)
 
     def error(l):
         target = jnp.where(lmap[l] == 0, hn[0, c, z].astype(F32), hn[1, c, z].astype(F32))
@@ -484,23 +489,44 @@
 
         loop(1024, 256, body)
 
-    def cuts(l, at, width, half):
-        lo, hi = max(at, half * WIDTH[l]), min(at + width, (half + 1) * WIDTH[l])
-        return [(lo, hi)] if lo < hi else []
-
-    def put(l, at, g):
+    def put(key, g, tile=0):
+        to = scatter[key]
+        for j in range(g.shape[1] // 128):
+            lo = to.base + 64 * (tile + j)
+            to.buf[:, :, lo:lo + 64, :] = g[:, 128 * j:128 * j + 128].reshape(4, 4, 64, 128).astype(BF)
+
+    def proj_grad():
+        put("p", contract_rows(blocks(xs, 0), delta[0]) + contract_rows(blocks(xs, 1), delta[1]))
+
+    def weight_grad(key, left, right):
+        for n in (0, 256):
+            put(key, dot(left[...], right[:, n:n + 256]), n // 128)
+        scatter[key].one()
+
+    def down_grad(l):
+        sn[l] = blocks(gnew, l)
+        gyt[...] = sn[l].T
+        weight_grad("d" + str(l), gyt, u_out.at[l])
+
+    def unit_grads(l):
+        weight_grad("g" + str(l), snt.at[l], ga.at[l])
+        weight_grad("u" + str(l), snt.at[l], gb.at[l])
+
+    found = {}
+
+    def grad_end(key):
+        out = {"d": down_out, "g": gate_out, "u": up_out, "p": proj_out}[key[0]]
+        out = out if key == "p" else out.at[int(key[1])]
         for half in (0, 1):
-            for lo, hi in cuts(l, at, g.shape[1], half):
-                v = g[:, lo - at:hi - at].reshape(4, 4, 64, hi - lo).astype(BF)
-                wg[1 - l, :, :, 64 * half:64 * half + 64, lo - half * WIDTH[l]:hi - half * WIDTH[l]] = v
-
-    def proj_grad():
-        g = contract_rows(blocks(xs, 0), delta[0]) + contract_rows(blocks(xs, 1), delta[1])
-        put(1, 1536, g)
+            g = scatter[key].five(half)
+            tiles = g.shape[0] // 64
+            for j in range(tiles):
+                at = 128 * (tiles * half + j)
+                out[:, at:at + 128] = g[64 * j:64 * j + 64]
+            v = jnp.sum(jnp.sum(g * g, axis=1, keepdims=True), axis=0, keepdims=True)
+            found[key[0]] = found[key[0]] + v if key[0] in found else v
 
     def units_back(l):
-        sn[l] = blocks(gnew, l)
-
         def body(n):
             cols = pl.ds(n, 256)
             du = contract_cols(sn[l], sd[l, cols, :])
@@ -529,27 +555,6 @@
                 gpart[0, i % 2, i // 2, rows, :] = p[:, i * 128:(i + 1) * 128].astype(BF)
 
         loop(256, 32, through)
-
-    def weight_grads(l):
-        gyt[...] = sn[l].T
-        for at, left, right in ((0, snt.at[l], ga), (512, snt.at[l], gb), (1024, gyt, u_out)):
-            for n in (0, 256):
-                put(l, at + n, dot(left[...], right[l, :, n:n + 256]))
-
-    def grads_end(l):
-        found = {}
-        for half in (0, 1):
-            g = scatter[l].five(half)
-            for out, lo, hi in ((gate_out, 0, 512), (up_out, 512, 1024), (down_out, 1024, 1536), (proj_out, 1536, 1792)):
-                for b, e in cuts(l, lo, hi - lo, half):
-                    v = g[:, b - half * WIDTH[l]:e - half * WIDTH[l]]
-                    if out is proj_out:
-                        out[:, b - lo:e - lo] = v
-                    else:
-                        out[l, :, b - lo:e - lo] = v
-                    v = jnp.sum(jnp.sum(v * v, axis=1, keepdims=True), axis=0, keepdims=True)
-                    found[lo] = found[lo] + v if lo in found else v
-        return [found[lo] for lo in sorted(found)]
 
     def totals(values):
         for i, v in enumerate(values):
@@ -578,44 +583,49 @@
     gu[0].first_forward()
     dn[0].first_forward()
     gu[0].second()
-    loads[2].wait()
+    loads[3].wait()
+    loads[4].wait()
     gu[1].first()
+    loads[5].wait()
+    dn[1].first()
+    dn[0].second()
     student(0)
-    dn[0].second()
     student_end(0)
     gu[0].second_forward()
     gu[1].first_forward()
+    dn[1].first_forward()
     student(1)
     student_end(1)
     dn[0].second_forward()
     gu[1].second()
-    loads[3].wait()
-    dn[1].first()
+    dn[1].second()
     gu[0].complete()
     teacher_up(0)
     dn[0].complete()
-    teacher_down(0)
+    teacher_down(0, 1 - c)
     tsum[0].across()
-    dn[1].first_forward()
+    teacher_down(0, c)
     tsum[0].along()
+    predict(0)
     teacher_result(0)
     tgather.along()
-    dn[1].second()
+    gu[1].second_forward()
+    predict(1)
     tgather.across()
     tgather.complete()
     teacher_norm(1)
-    gu[1].second_forward()
-    predict(0)
-    predict(1)
+    dn[1].second_forward()
     for i in range(8):
         states_out[0, :, i * 256:(i + 1) * 256] = hn[0, i % 2, i // 2, pl.ds(pl.multiple_of(t * 32, 32), 32), :]
-    dn[1].second_forward()
     gu[1].complete()
     teacher_up(1)
     dn[1].complete()
-    teacher_down(1)
+    teacher_down(1, 1 - c)
     tsum[1].across()
+    teacher_down(1, c)
     tsum[1].along()
+    gu[0].sent()
+    gu[1].sent()
     teacher_result(1)
     e1 = error(1)
     top_part()
@@ -629,49 +639,91 @@
         where = {"tensor_0": o // 2, "tensor_1": lax.rem(o, 2)}
         shared.append(copies.start(copies.tags(1)[0], hn.at[1, c, z, rows], rows_in.at[t], where))
     rows_in[t] = hn[1, c, z, pl.ds(pl.multiple_of(t * 32, 32), 32), :]
-    gu[0].sent()
     proj_grad()
+    scatter["p"].one()
     gwide[...] = gsum[1].total()
     gnew[1, c, z] = gwide[...].astype(BF)
     ggather[1].along()
+    scatter["p"].two()
     ggather[1].across()
     ggather[1].complete()
+    down_grad(1)
     units_back(1)
     norm_part()
     gsum[0].across()
-    weight_grads(1)
-    scatter[1].one()
+    unit_grads(1)
     gsum[0].along()
-    scatter[1].two()
+    scatter["p"].three()
+    scatter["d1"].two()
     gwide[...] = gwide[...] + gsum[0].total()
     gnew[0, c, z] = gwide[...].astype(BF)
     ggather[0].along()
+    scatter["g1"].two()
+    scatter["u1"].two()
     ggather[0].across()
+    scatter["p"].four()
+    scatter["d1"].three()
     ggather[0].complete()
+    down_grad(0)
     units_back(0)
-    gu[1].sent()
-    weight_grads(0)
-    scatter[0].one()
-    scatter[1].three()
-    scatter[0].two()
-    scatter[1].four()
-    scatter[0].three()
-    found = grads_end(1)
-    scatter[0].four()
+    unit_grads(0)
+    scatter["g1"].three()
+    scatter["u1"].three()
+    scatter["d0"].two()
+    scatter["d1"].four()
+    scatter["g0"].two()
+    scatter["g1"].four()
+    scatter["u0"].two()
+    scatter["u1"].four()
+    grad_end("p")
+    grad_end("d1")
+    scatter["d0"].three()
+    grad_end("g1")
+    scatter["g0"].three()
+    grad_end("u1")
     for copy in shared:
         copy.wait_recv()
     for i in range(8):
         states_out[1, :, i * 256:(i + 1) * 256] = rows_in[i]
-    more = grads_end(0)
-    found = [found[i] + more[i] for i in range(3)] + found[3:]
-    total = totals([e0, e1] + found)
+    scatter["u0"].three()
+    scatter["d0"].four()
+    scatter["g0"].four()
+    scatter["u0"].four()
+    grad_end("d0")
+    grad_end("g0")
+    grad_end("u0")
+    total = totals([e0, e1] + [found[k] for k in "gudp"])
     mean_out[0:2, :] = total[0:2] / float(4096 * DT)
     mean_out[2:5, :] = jnp.sqrt(total[2:5] / float(S_LAYERS * DS * FS))
     mean_out[5:8, :] = jnp.sqrt(total[5:8] / float(DS * DT))
     copies.finish()
 
 
-def run(lmap, tin, tgain, sin, sgain, gu, dn, sg, su, sd, proj):
+def finish_kernel(stats, *refs):
+    ins, outs, mean, rms = refs[:5], refs[5:10], refs[10], refs[11]
+    for src, dst in zip(ins, outs):
+        dst[...] = src[...]
+    for i in range(2):
+        mean[i] = stats[i, 0]
+    for i in range(4):
+        rms[i] = stats[2 + i, 0]
+
+
+def finish(states, gate, up, down, width, stats):
+    arrays = (states, gate, up, down, width)
+    here = pl.BlockSpec(memory_space=VMEM)
+    scalars = pl.BlockSpec(memory_space=pltpu.SMEM)
+    return pl.pallas_call(
+        finish_kernel,
+        out_shape=tuple(jax.ShapeDtypeStruct(a.shape, a.dtype) for a in arrays)
+        + (jax.ShapeDtypeStruct((2,), F32), jax.ShapeDtypeStruct((4,), F32)),
+        in_specs=[scalars] + [here] * 5,
+        out_specs=(here,) * 5 + (scalars,) * 2,
+        name="finish",
+    )(stats, *arrays)
+
+
+def run(lmap, tin, tgain, sin, sgain, gate, up, dn, sg, su, sd, proj):
     shape = jax.ShapeDtypeStruct
     here = pl.BlockSpec(memory_space=VMEM)
     away = pl.BlockSpec(memory_space=pl.ANY)
@@ -685,10 +737,10 @@
             shape((64, 256), F32),
             shape((8, 128), F32),
         ),
-        in_specs=[pl.BlockSpec(memory_space=pltpu.SMEM)] + [here] * 4 + [away] * 6,
+        in_specs=[pl.BlockSpec(memory_space=pltpu.SMEM)] + [here] * 4 + [away] * 7,
         out_specs=(here,) * 6,
         scratch_shapes=[
-            VMEM((2, 4, 4, 128, 1408), BF),
+            VMEM((2, 4, 4, 1376, 128), BF),
             VMEM((2, 4, 4, 688, 128), BF),
             VMEM((2, 1024, 512), BF),
             VMEM((2, 1024, 512), BF),
@@ -696,7 +748,7 @@
             VMEM((1024, 256), BF),
             VMEM((2, 2, 4, 256, 128), BF),
             VMEM((256, 2048), BF),
-            VMEM((256, 1408), F32),
+            VMEM((256, 1024), F32),
             VMEM((256, 768), BF),
             VMEM((2, 256, 1024), BF),
             VMEM((2, 1024, 256), BF),
@@ -728,8 +780,8 @@
         ]
         + [
             VMEM(s, BF)
-            for w in (896, 768)
-            for s in ((2, 2, 2, 64, w), (2, 2, 4, 64, w), (2, 2, 32, w), (2, 2, 64, w))
+            for _, _, _, r in CHUNKS
+            for s in ((2, 2, 2, r, 128), (2, 2, 4, r, 128), (2, 2, r // 2, 128), (2, 2, r, 128))
         ]
         + [
             VMEM((4, 8, 128), F32),
@@ -744,22 +796,19 @@
             collective_id=0, has_side_effects=True, vmem_limit_bytes=67043328
         ),
         name="step",
-    )(lmap, tin, tgain, sin, sgain, gu, dn, sg, su, sd, proj)
+    )(lmap, tin, tgain, sin, sgain, gate, up, dn, sg, su, sd, proj)
 
 
 def per_device(
     teacher_in, teacher_gain, t_gate, t_up, t_down,
     student_in, student_gain, s_gate, s_up, s_down, proj, layer_map,
 ):
-    zeros = jnp.zeros((T_LAYERS, 128, 20), BF)
-    gu = jnp.concatenate(
-        [t_gate[:, :, :640], t_up[:, :, :640], t_gate[:, :, 640:], zeros, t_up[:, :, 640:], zeros], axis=2
+    own_states, gate, up, down, width, stats = run(
+        layer_map, teacher_in, teacher_gain, student_in, student_gain,
+        jnp.swapaxes(t_gate, 1, 2), jnp.swapaxes(t_up, 1, 2), t_down, s_gate, s_up, s_down, proj,
     )
-    dn = jnp.pad(t_down, ((0, 0), (0, 4), (0, 0)))
-    own_states, gate, up, down, width, stats = run(
-        layer_map, teacher_in, teacher_gain, student_in, student_gain, gu, dn, s_gate, s_up, s_down, proj
-    )
-    return (own_states, gate, up, jnp.swapaxes(down, 1, 2), width, stats[0:2, 0], stats[2:6, 0])
+    own_states, gate, up, down, width, mean_error, grad_rms = finish(own_states, gate, up, down, width, stats)
+    return (own_states, gate, up, jnp.swapaxes(down, 1, 2), width, mean_error, grad_rms)
 
 
 def solution(mesh):

time: 220 us -> 190 us (0.86)
  Pallas kernels: 202 us -> 185 us
  local copies, waits for them, and re-layouts: 16.7 us -> 3.79 us
    pallas_call x1, Pallas kernels: 202 us -> 183 us  [run(): pl.pallas_call(step_kernel, out_shape=(shape((2, 32, 2048), BF), shape((2...]
    unnamed x14 -> x1, local copies, waits for them, and re-layouts: 9.44 us -> 1.76 us
    slice x7 -> x0, local copies, waits for them, and re-layouts: 5.46 us -> none  [the longest x1 1.34 us: per_device(): stats[2:6, 0]]
    pallas_call x0 -> x1, Pallas kernels: none -> 2.21 us  [finish(): pl.pallas_call(finish_kernel, out_shape=tuple((jax.ShapeDtypeStruct(a.sha...]
where the time goes in v3:
time: 190 us; the launch traced here: 189 us
  Pallas kernels  185 us (97%)
  local copies, waits for them, and re-layouts  3.79 us (2%)
    pallas_call x1, Pallas kernels, run(): pl.pallas_call(step_kernel, out_shape=(shape((2, 32, 2048), BF), shape((2...  183 us

profile of v3, /device:TPU:1, one launch (start us, length us, event | category | flops | bytes accessed | tf_op | source)
XLA Modules:
  0.0 189.5 jit_solution(3870980895657004905)
XLA Ops:
  0.6 1.8 copy.21.dn_in
  2.4 2.0 %copy_bitcast_fusion = (bf16[2,684,128]{2,1,0:T(8,128)(2,1)}, bf16[2,684,128]{2,1,0:T(8,128)(2,1)}) fusion(bf16[2,128,684]{1,0,2:T(2,128)(2,1)} %param.15, bf16[2,128,684]{1,0,2:T(2,128)(2,1)} %param.14), kind=kLoop, calls=%fused_computation | loop fusion | bytes 1400832 | tf_op jit(solution)/shard_map/transpose | solution.py:808
  4.4 182.9 %step.1 = (bf16[2,32,2048]{2,1,0:T(8,128)(2,1)}, f32[2,64,512]{2,1,0:T(8,128)}, f32[2,64,512]{2,1,0:T(8,128)}, f32[2,64,512]{2,1,0:T(8,128)}, f32[64,256]{1,0:T(8,128)}, /*index=5*/f32[8,128]{1,0:T(8,128)}) custom-call(s32[2]{0:T(128)} %lmap.1, bf16[256,2048]{1,0:T(8,128)(2,1)} %tin.1, f32[2,2048]{1,0:T(2,128)} %tgain.1, bf16[256,1024]{1,0:T(8,128)(2,1)} %sin.1, ...), custom_call_target="tpu_custom_call" | custom-call | tf_op jit(solution)/shard_map/step/pallas_call | solution.py:730
  187.3 2.2 %finish.1 = (bf16[2,32,2048]{2,1,0:T(8,128)(2,1)}, f32[2,64,512]{2,1,0:T(8,128)}, f32[2,64,512]{2,1,0:T(8,128)}, f32[2,64,512]{2,1,0:T(8,128)}, f32[64,256]{1,0:T(8,128)}, /*index=5*/f32[2]{0:T(128)}, f32[4]{0:T(128)}) custom-call(f32[8,128]{1,0:T(8,128)} %get-tuple-element.20.stats, bf16[2,32,2048]{2,1,0:T(8,128)(2,1)} %get-tuple-element.21.refs_0_, ...), custom_call_target="tpu_custom_call" | custom-call | tf_op jit(solution)/shard_map/finish/pallas_call | solution.py:716

commit v4 on v3

--- a/solution.py
+++ b/solution.py
@@ -21,7 +21,7 @@
 MESH = pl.DeviceIdType.MESH
 BF = jnp.bfloat16
 F32 = jnp.float32
-N_COPY = 244
+N_COPY = 260
 N_LOCAL = 11
 GU_HALVES = ((0, 352, 688), (688, 1040, 1376))
 CHUNKS = (
@@ -315,6 +315,22 @@
         return mine[...].astype(F32) + r4[half, 0].astype(F32) + r4[half, 1].astype(F32)
 
 
+class RingGather(TensorGather):
+    def along(self):
+        mine = self.buf.at[self.core, self.z]
+        self.o = [
+            self.c.start(self.c.tags(1)[0], mine, mine, {"tensor_0": lax.rem(self.z + k, 4)}) for k in (1, 3)
+        ]
+
+    def forward(self):
+        half = self.buf.shape[2] // 2
+        self.s = []
+        for copy, k, lo in zip(self.o, (1, 3), (0, half)):
+            copy.wait_recv()
+            piece = self.buf.at[self.core, lax.rem(self.z + 4 - k, 4), pl.ds(lo, half)]
+            self.s.append(self.c.start(self.c.tags(1)[0], piece, piece, {"tensor_0": lax.rem(self.z + k, 4)}))
+
+
 def blocks(ref, *lead, rows=slice(None)):
     return jnp.concatenate([ref[lead + (t % 2, t // 2, rows)] for t in range(8)], axis=1)
 
@@ -322,16 +338,19 @@
 def step_kernel(
     lmap, tin, tgain, sin, sgain, gate_in, up_in, dn_in, sg_in, su_in, sd_in, proj_in,
     states_out, gate_out, up_out, down_out, proj_out, mean_out,
-    wg, wd, sg, su, sd, proj, xs, tn, acts, hid, sn, snt, a_out, b_out, u_out,
+    wg, wd, sg, su, sd, pf, xs, tn, acts, hid, sn, snt, a_out, b_out, u_out,
     spart, spair, sboth, sring, tpart, tpair, tboth, tring, hn, rows_in,
-    pred, delta, gpart, gpair, gboth, gring, gnew, gwide, gyt, ga, gb, side, *rest,
+    pred, delta, gpart, gpair, gboth, gring, gnew, gwide, gyt, ga, gb, base, *rest,
 ):
-    sums, (stat, stat_y, stat_x, stat_t, send, recv, local) = rest[:-7], rest[-7:]
+    sums, (stat, stat_p, stat_t, send, recv, local) = rest[:-6], rest[-6:]
     y, x = lax.axis_index("dp_0"), lax.axis_index("dp_1")
     z, c = lax.axis_index("tensor_0"), lax.axis_index("tensor_1")
     t = 2 * z + c
-    peers = [{"dp_0": lax.rem(y + k, 4)} for k in (1, 2, 3)]
-    peers += [{"dp_1": lax.rem(x + k, 4)} for k in (1, 2, 3)]
+    plane = [
+        {"dp_0": lax.rem(y + k // 4, 4), "dp_1": lax.rem(x + k % 4, 4)}
+        for k in (10, 6, 9, 11, 14, 2, 8, 5, 7, 13, 15, 1, 3, 4, 12)
+    ]
+    peers = list(plane)
     others = [lax.rem(t + k, 8) for k in range(1, 8)]
     peers += [{"tensor_0": o // 2, "tensor_1": lax.rem(o, 2)} for o in others]
     barrier = pltpu.get_barrier_semaphore()
@@ -357,7 +376,7 @@
     load(sg_in, sg)
     load(su_in, su)
     load(sd_in, sd)
-    load(proj_in, proj)
+    load(proj_in, pf.at[c, z])
     gu = [Gather(copies, wg.at[l], GU_HALVES, y, x) for l in (0, 1)]
     dn = [Gather(copies, wd.at[l], DN_HALVES, y, x) for l in (0, 1)]
     pl.semaphore_wait(barrier, len(peers))
@@ -422,6 +441,7 @@
 
         lax.fori_loop(0, 4, body, 0)
 
+    pgather = RingGather(copies, pf, z, c)
     ssum = [TensorSum(copies, spart.at[l], spair.at[l], sboth.at[l], sring.at[l], z, c) for l in (0, 1)]
     sgather = [TensorGather(copies, xs.at[l], z, c) for l in (0, 1)]
     tsum = [TensorSum(copies, tpart.at[k], tpair.at[k], tboth.at[k], tring.at[k], z, c) for k in (0, 1)]
@@ -443,13 +463,13 @@
         hn[k, c, z] = new
 
     def predict(l):
-        pred[l] = dot(blocks(xs, l), proj[...])
+        pred[l] = dot(blocks(xs, l), pf[c, z])
         snt[l] = sn[l].T
 
     def student(l):
         student_norm(l)
         if l == 0:
-            for copy in loads[6:10]:
+            for copy in loads[6:9]:
                 copy.wait()
         student_units(l)
         student_part(l)
@@ -465,8 +485,8 @@
     gsum = [TensorSum(copies, gpart.at[l], gpair.at[l], gboth.at[l], gring.at[l], z, c) for l in (0, 1)]
     ggather = [TensorGather(copies, gnew.at[l], z, c) for l in (0, 1)]
     scatter = {}
-    for i, (key, k, base, rows) in enumerate(CHUNKS):
-        scatter[key] = ScatterSum(copies, wg.at[k], base, rows, sums[4 * i:4 * i + 4], y, x)
+    for i, (key, k, first, rows) in enumerate(CHUNKS):
+        scatter[key] = ScatterSum(copies, wg.at[k], first, rows, sums[4 * i:4 * i + 4], y, x)
 
     def error(l):
         target = jnp.where(lmap[l] == 0, hn[0, c, z].astype(F32), hn[1, c, z].astype(F32))
@@ -474,20 +494,30 @@
         delta[l] = (e * (2.0 / (S_LAYERS * SEQ))).astype(BF)
         return jnp.sum(jnp.sum(e * e, axis=1, keepdims=True), axis=0, keepdims=True)
 
+    def base_part(l):
+        base[l] = jnp.zeros((256, 128), F32)
+        own = pl.ds(pl.multiple_of(t * 128, 128), 128)
+
+        def body(i, carry):
+            for half in (0, 1):
+                e = dot(blocks(xs, l), pf[half, i]) - hn[0, half, i].astype(F32)
+                delta[half] = (e * (2.0 / (S_LAYERS * SEQ))).astype(BF)
+                base[l] += contract_cols(delta[half], pf[half, i, own, :])
+            return carry
+
+        lax.fori_loop(0, 4, body, 0)
+
     def top_part():
+        products = blocks(tpart, 1)
+
         def body(i, carry):
-            p = contract_cols(delta[1], proj[pl.ds(pl.multiple_of(i * 256, 256), 256), :])
+            rows = pl.ds(pl.multiple_of(i * 256, 256), 256)
+            p = contract_cols(products, blocks(pf, rows=rows)) * (2.0 / (S_LAYERS * SEQ))
             gpart[1, 0, i] = p[:, :128].astype(BF)
             gpart[1, 1, i] = p[:, 128:].astype(BF)
             return carry
 
         lax.fori_loop(0, 4, body, 0)
-
-    def side_part():
-        def body(n):
-            side[:, pl.ds(n, 256)] = contract_cols(delta[0], proj[pl.ds(n, 256), :])
-
-        loop(1024, 256, body)
 
     def put(key, g, tile=0):
         to = scatter[key]
@@ -504,7 +534,6 @@
         scatter[key].one()
 
     def down_grad(l):
-        sn[l] = blocks(gnew, l)
         gyt[...] = sn[l].T
         weight_grad("d" + str(l), gyt, u_out.at[l])
 
@@ -535,7 +564,8 @@
             ga[l, :, cols] = (du * b * s * (1.0 + a * (1.0 - s))).astype(BF)
             gb[l, :, cols] = (du * (a * s)).astype(BF)
 
-        loop(512, 256, body)
+        for n in (0, 256):
+            body(n)
 
     def norm_part():
         def body(n):
@@ -550,7 +580,7 @@
             scale = inverse_rms(v)
             q = acts[rows, 0:1024] * sgain[1:2, :]
             m = jnp.mean(v * q, axis=-1, keepdims=True)
-            p = scale * q - v * (scale * scale * scale) * m + side[rows, :]
+            p = scale * q - v * (scale * scale * scale) * m
             for i in range(8):
                 gpart[0, i % 2, i // 2, rows, :] = p[:, i * 128:(i + 1) * 128].astype(BF)
 
@@ -561,9 +591,8 @@
             stat[0, i:i + 1, :] = jnp.broadcast_to(v, (1, 128))
         stat[0, 6:8, :] = jnp.zeros((2, 128), F32)
         steps = (
-            (stat_y, y, [(lax.rem(y + k, 4), {"dp_0": lax.rem(y + k, 4)}) for k in (2, 1, 3)]),
-            (stat_x, x, [(lax.rem(x + k, 4), {"dp_1": lax.rem(x + k, 4)}) for k in (2, 1, 3)]),
-            (stat_t, t, [(o, {"tensor_0": o // 2, "tensor_1": lax.rem(o, 2)}) for o in others]),
+            (stat_p, 4 * y + x, [(0, where) for where in plane]),
+            (stat_t, t, [(0, {"tensor_0": o // 2, "tensor_1": lax.rem(o, 2)}) for o in others]),
         )
         for i, (got, me, targets) in enumerate(steps):
             sent = [
@@ -579,6 +608,8 @@
             stat[i + 1] = total
         return total
 
+    loads[9].wait()
+    pgather.along()
     teacher_norm(0)
     gu[0].first_forward()
     dn[0].first_forward()
@@ -590,12 +621,15 @@
     dn[1].first()
     dn[0].second()
     student(0)
+    pgather.forward()
     student_end(0)
+    pgather.across()
     gu[0].second_forward()
     gu[1].first_forward()
     dn[1].first_forward()
     student(1)
     student_end(1)
+    pgather.complete()
     dn[0].second_forward()
     gu[1].second()
     dn[1].second()
@@ -615,24 +649,44 @@
     tgather.complete()
     teacher_norm(1)
     dn[1].second_forward()
+    base_part(0)
+    base_part(1)
     for i in range(8):
         states_out[0, :, i * 256:(i + 1) * 256] = hn[0, i % 2, i // 2, pl.ds(pl.multiple_of(t * 32, 32), 32), :]
     gu[1].complete()
     teacher_up(1)
     dn[1].complete()
-    teacher_down(1, 1 - c)
+    teacher_down(1, 0)
+    teacher_down(1, 1)
+    top_part()
+    gsum[1].across()
     tsum[1].across()
-    teacher_down(1, c)
-    tsum[1].along()
+    gsum[1].along()
     gu[0].sent()
     gu[1].sent()
+    late = gsum[1].total()
+    gwide[...] = base[1] - jnp.where(lmap[1] == 1, late, 0.0)
+    gnew[1, c, z] = gwide[...].astype(BF)
+    ggather[1].along()
+    tsum[1].along()
+    gwide[...] = gwide[...] + base[0] - jnp.where(lmap[0] == 1, late, 0.0)
+    ggather[1].across()
+    ggather[1].complete()
+    sn[1] = blocks(gnew, 1)
+    down_grad(1)
+    units_back(1)
+    norm_part()
+    gsum[0].across()
+    unit_grads(1)
+    gsum[0].along()
+    scatter["d1"].two()
+    gwide[...] = gwide[...] + gsum[0].total()
+    gnew[0, c, z] = gwide[...].astype(BF)
+    ggather[0].along()
+    scatter["g1"].two()
     teacher_result(1)
     e1 = error(1)
-    top_part()
-    gsum[1].across()
     e0 = error(0)
-    side_part()
-    gsum[1].along()
     shared = []
     for o in others:
         rows = pl.ds(pl.multiple_of(o * 32, 32), 32)
@@ -641,42 +695,27 @@
     rows_in[t] = hn[1, c, z, pl.ds(pl.multiple_of(t * 32, 32), 32), :]
     proj_grad()
     scatter["p"].one()
-    gwide[...] = gsum[1].total()
-    gnew[1, c, z] = gwide[...].astype(BF)
-    ggather[1].along()
-    scatter["p"].two()
-    ggather[1].across()
-    ggather[1].complete()
-    down_grad(1)
-    units_back(1)
-    norm_part()
-    gsum[0].across()
-    unit_grads(1)
-    gsum[0].along()
-    scatter["p"].three()
-    scatter["d1"].two()
-    gwide[...] = gwide[...] + gsum[0].total()
-    gnew[0, c, z] = gwide[...].astype(BF)
-    ggather[0].along()
-    scatter["g1"].two()
     scatter["u1"].two()
     ggather[0].across()
-    scatter["p"].four()
     scatter["d1"].three()
+    scatter["p"].two()
     ggather[0].complete()
+    sn[0] = blocks(gnew, 0)
     down_grad(0)
     units_back(0)
     unit_grads(0)
+    scatter["p"].three()
+    scatter["d1"].four()
     scatter["g1"].three()
     scatter["u1"].three()
     scatter["d0"].two()
-    scatter["d1"].four()
+    scatter["p"].four()
     scatter["g0"].two()
     scatter["g1"].four()
     scatter["u0"].two()
     scatter["u1"].four()
+    grad_end("d1")
     grad_end("p")
-    grad_end("d1")
     scatter["d0"].three()
     grad_end("g1")
     scatter["g0"].three()
@@ -745,7 +784,7 @@
             VMEM((2, 1024, 512), BF),
             VMEM((2, 1024, 512), BF),
             VMEM((2, 512, 1024), BF),
-            VMEM((1024, 256), BF),
+            VMEM((2, 4, 1024, 256), BF),
             VMEM((2, 2, 4, 256, 128), BF),
             VMEM((256, 2048), BF),
             VMEM((256, 1024), F32),
@@ -776,7 +815,7 @@
             VMEM((1024, 256), BF),
             VMEM((2, 256, 512), BF),
             VMEM((2, 256, 512), BF),
-            VMEM((256, 1024), F32),
+            VMEM((2, 256, 128), F32),
         ]
         + [
             VMEM(s, BF)
@@ -784,9 +823,8 @@
             for s in ((2, 2, 2, r, 128), (2, 2, 4, r, 128), (2, 2, r // 2, 128), (2, 2, r, 128))
         ]
         + [
-            VMEM((4, 8, 128), F32),
-            VMEM((4, 8, 128), F32),
-            VMEM((4, 8, 128), F32),
+            VMEM((3, 8, 128), F32),
+            VMEM((16, 8, 128), F32),
             VMEM((8, 8, 128), F32),
             pltpu.SemaphoreType.DMA((N_COPY,)),
             pltpu.SemaphoreType.DMA((N_COPY,)),

time: 190 us -> 185 us (0.974)
  Pallas kernels: 185 us -> 181 us
    pallas_call x1, Pallas kernels: 183 us -> 178 us  [run(): pl.pallas_call(step_kernel, out_shape=(shape((2, 32, 2048), BF), shape((2...]
where the time goes in v4:
time: 185 us
  Pallas kernels  181 us (98%)
  local copies, waits for them, and re-layouts  3.79 us (2%)
    pallas_call x1, Pallas kernels, run(): pl.pallas_call(step_kernel, out_shape=(shape((2, 32, 2048), BF), shape((2...  178 us

profile of v4, /device:TPU:1, one launch (start us, length us, event | category | flops | bytes accessed | tf_op | source)
XLA Modules:
  0.0 185.1 jit_solution(12536408520284728914)
XLA Ops:
  0.6 1.8 copy.21.dn_in
  2.4 2.0 %copy_bitcast_fusion = (bf16[2,684,128]{2,1,0:T(8,128)(2,1)}, bf16[2,684,128]{2,1,0:T(8,128)(2,1)}) fusion(bf16[2,128,684]{1,0,2:T(2,128)(2,1)} %param.15, bf16[2,128,684]{1,0,2:T(2,128)(2,1)} %param.14), kind=kLoop, calls=%fused_computation | loop fusion | bytes 1400832 | tf_op jit(solution)/shard_map/transpose | solution.py:846
  4.4 178.3 %step.1 = (bf16[2,32,2048]{2,1,0:T(8,128)(2,1)}, f32[2,64,512]{2,1,0:T(8,128)}, f32[2,64,512]{2,1,0:T(8,128)}, f32[2,64,512]{2,1,0:T(8,128)}, f32[64,256]{1,0:T(8,128)}, /*index=5*/f32[8,128]{1,0:T(8,128)}) custom-call(s32[2]{0:T(128)} %lmap.1, bf16[256,2048]{1,0:T(8,128)(2,1)} %tin.1, f32[2,2048]{1,0:T(2,128)} %tgain.1, bf16[256,1024]{1,0:T(8,128)(2,1)} %sin.1, ...), custom_call_target="tpu_custom_call" | custom-call | tf_op jit(solution)/shard_map/step/pallas_call | solution.py:769
  182.7 2.2 %finish.1 = (bf16[2,32,2048]{2,1,0:T(8,128)(2,1)}, f32[2,64,512]{2,1,0:T(8,128)}, f32[2,64,512]{2,1,0:T(8,128)}, f32[2,64,512]{2,1,0:T(8,128)}, f32[64,256]{1,0:T(8,128)}, /*index=5*/f32[2]{0:T(128)}, f32[4]{0:T(128)}) custom-call(f32[8,128]{1,0:T(8,128)} %get-tuple-element.20.stats, bf16[2,32,2048]{2,1,0:T(8,128)(2,1)} %get-tuple-element.21.refs_0_, ...), custom_call_target="tpu_custom_call" | custom-call | tf_op jit(solution)/shard_map/finish/pallas_call | solution.py:755

commit v5 on v4

--- a/solution.py
+++ b/solution.py
@@ -21,7 +21,8 @@
 MESH = pl.DeviceIdType.MESH
 BF = jnp.bfloat16
 F32 = jnp.float32
-N_COPY = 260
+N_SEND = 64
+N_RECV = 110
 N_LOCAL = 11
 GU_HALVES = ((0, 352, 688), (688, 1040, 1376))
 CHUNKS = (
@@ -67,39 +68,52 @@
 
 class Copies:
     def __init__(self, send, recv):
-        self.send, self.recv, self.used, self.made = send, recv, 0, []
-
-    def tags(self, count):
-        first = self.used
-        self.used += count
-        return list(range(first, first + count))
-
-    def start(self, tag, src, dst, where):
+        self.send, self.recv, self.groups, self.made = send, recv, 0, []
+
+    def group(self):
+        self.groups += 1
+        assert self.groups <= N_RECV
+        return self.groups - 1
+
+    def start(self, group, src, dst, where):
+        slot = len(self.made) % N_SEND
+        if len(self.made) >= N_SEND:
+            self.sent([self.made[len(self.made) - N_SEND]])
         copy = pltpu.make_async_remote_copy(
             src_ref=src,
             dst_ref=dst,
-            send_sem=self.send.at[tag],
-            recv_sem=self.recv.at[tag],
+            send_sem=self.send.at[slot],
+            recv_sem=self.recv.at[group],
             device_id=where,
             device_id_type=MESH,
         )
         copy.start()
-        self.made.append(copy)
-        return copy
+        self.made.append([copy, False])
+        return self.made[-1]
+
+    def arrived(self, group, ref, where):
+        pltpu.make_async_remote_copy(
+            src_ref=ref,
+            dst_ref=ref,
+            send_sem=self.send.at[0],
+            recv_sem=self.recv.at[group],
+            device_id=where,
+            device_id_type=MESH,
+        ).wait_recv()
 
     def sent(self, some):
-        for copy in some:
-            copy.wait_send()
-        self.made = [copy for copy in self.made if all(copy is not done for done in some)]
+        for entry in some:
+            if not entry[1]:
+                entry[0].wait_send()
+                entry[1] = True
 
     def finish(self):
-        for copy in self.made:
-            copy.wait_send()
+        self.sent(self.made)
 
 
 class Gather:
     def __init__(self, copies, buf, halves, y, x):
-        self.c, self.buf, self.halves, self.y, self.x = copies, buf, halves, y, x
+        self.c, self.buf, self.halves, self.y, self.x, self.copies = copies, buf, halves, y, x, []
 
     def slab(self, half, outer, inner, lo, hi):
         r = pl.ds(lo, hi - lo)
@@ -109,6 +123,12 @@
         if half == 0:
             return "dp_1", self.x, "dp_0", self.y
         return "dp_0", self.y, "dp_1", self.x
+
+    def both(self, up, down, axis, pos):
+        group = self.c.group()
+        for piece, k in ((up, 1), (down, 3)):
+            self.copies.append(self.c.start(group, piece, piece, {axis: lax.rem(pos + k, 4)}))
+        return group
 
     def first(self):
         self.own = []
@@ -116,44 +136,25 @@
             a, pa, _, pb = self.axes(half)
             lo, _, hi = self.halves[half]
             mine = self.slab(half, pb, pa, lo, hi)
-            t = self.c.tags(2)
-            self.own.append(
-                (
-                    self.c.start(t[0], mine, mine, {a: lax.rem(pa + 1, 4)}),
-                    self.c.start(t[1], mine, mine, {a: lax.rem(pa + 3, 4)}),
-                )
-            )
+            self.own.append(self.both(mine, mine, a, pa))
 
     def first_forward(self):
         self.fwd = []
         for half in (0, 1):
             a, pa, _, pb = self.axes(half)
             lo, mid, hi = self.halves[half]
+            self.c.arrived(self.own[half], self.slab(half, pb, pl.ds(0, 2), lo, hi), {a: lax.rem(pa + 1, 4)})
             up, down = lax.rem(pa + 1, 4), lax.rem(pa + 3, 4)
-            t = self.c.tags(2)
-            self.own[half][0].wait_recv()
-            piece = self.slab(half, pb, down, lo, mid)
-            f0 = self.c.start(t[0], piece, piece, {a: up})
-            self.own[half][1].wait_recv()
-            piece = self.slab(half, pb, up, mid, hi)
-            f1 = self.c.start(t[1], piece, piece, {a: down})
-            self.fwd.append((f0, f1))
+            self.fwd.append(self.both(self.slab(half, pb, down, lo, mid), self.slab(half, pb, up, mid, hi), a, pa))
 
     def second(self):
         self.row = []
         for half in (0, 1):
-            _, _, b, pb = self.axes(half)
+            a, pa, b, pb = self.axes(half)
             lo, _, hi = self.halves[half]
-            self.fwd[half][0].wait_recv()
-            self.fwd[half][1].wait_recv()
-            t = self.c.tags(2)
+            self.c.arrived(self.fwd[half], self.slab(half, pb, lax.rem(pa + 2, 4), lo, hi), {a: lax.rem(pa + 1, 4)})
             mine = self.slab(half, pb, pl.ds(0, 4), lo, hi)
-            self.row.append(
-                (
-                    self.c.start(t[0], mine, mine, {b: lax.rem(pb + 1, 4)}),
-                    self.c.start(t[1], mine, mine, {b: lax.rem(pb + 3, 4)}),
-                )
-            )
+            self.row.append(self.both(mine, mine, b, pb))
 
     def second_forward(self):
         self.last = []
@@ -161,78 +162,105 @@
             _, _, b, pb = self.axes(half)
             lo, _, hi = self.halves[half]
             up, down = lax.rem(pb + 1, 4), lax.rem(pb + 3, 4)
-            t = self.c.tags(2)
-            self.row[half][0].wait_recv()
-            piece = self.slab(half, down, pl.ds(0, 2), lo, hi)
-            f0 = self.c.start(t[0], piece, piece, {b: up})
-            self.row[half][1].wait_recv()
-            piece = self.slab(half, up, pl.ds(2, 2), lo, hi)
-            f1 = self.c.start(t[1], piece, piece, {b: down})
-            self.last.append((f0, f1))
+            self.c.arrived(self.row[half], self.slab(half, pl.ds(0, 2), pl.ds(0, 4), lo, hi), {b: up})
+            self.last.append(
+                self.both(
+                    self.slab(half, down, pl.ds(0, 2), lo, hi), self.slab(half, up, pl.ds(2, 2), lo, hi), b, pb
+                )
+            )
 
     def complete(self):
-        for pair in self.last:
-            for copy in pair:
-                copy.wait_recv()
+        for half in (0, 1):
+            _, _, b, pb = self.axes(half)
+            lo, _, hi = self.halves[half]
+            far = self.slab(half, lax.rem(pb + 2, 4), pl.ds(0, 4), lo, hi)
+            self.c.arrived(self.last[half], far, {b: lax.rem(pb + 1, 4)})
 
     def sent(self):
-        self.c.sent([copy for pair in self.own + self.fwd + self.row + self.last for copy in pair])
+        self.c.sent(self.copies)
 
 
 class TensorSum:
-    def __init__(self, copies, part, pair, both, ring, z, c):
+    def __init__(self, copies, part, pair, both, ring, z, c, lo=0, count=256):
         self.c, self.part, self.pair, self.both, self.ring = copies, part, pair, both, ring
-        self.z, self.core = z, c
+        self.z, self.core, self.rows = z, c, pl.ds(lo, count)
 
     def across(self):
         other = 1 - self.core
-        self.x = self.c.start(self.c.tags(1)[0], self.part.at[other], self.pair, {"tensor_1": other})
+        self.x = self.c.group()
+        src = self.part.at[other, pl.ds(0, 4), self.rows]
+        self.c.start(self.x, src, self.pair.at[pl.ds(0, 4), self.rows], {"tensor_1": other})
 
     def along(self):
-        self.x.wait_recv()
-        rows = self.part.shape[2]
+        self.c.arrived(self.x, self.pair.at[pl.ds(0, 4), self.rows], {"tensor_1": 1 - self.core})
         for k in range(4):
-            self.both[k] = (self.part[self.core, k].astype(F32) + self.pair[k].astype(F32)).astype(BF)
-        self.s = []
+            mine = self.part[self.core, k, self.rows].astype(F32) + self.pair[k, self.rows].astype(F32)
+            self.both[k, self.rows] = mine.astype(BF)
+        self.s = self.c.group()
         for k in (2, 1, 3):
             to = lax.rem(self.z + k, 4)
-            self.s.append(
-                self.c.start(self.c.tags(1)[0], self.both.at[to], self.ring.at[self.z], {"tensor_0": to})
-            )
+            self.c.start(self.s, self.both.at[to, self.rows], self.ring.at[self.z, self.rows], {"tensor_0": to})
 
     def total(self):
-        for copy in self.s:
-            copy.wait_recv()
-        acc = self.both[self.z].astype(F32)
+        self.c.arrived(self.s, self.ring.at[pl.ds(0, 3), self.rows], {"tensor_0": lax.rem(self.z + 1, 4)})
+        acc = self.both[self.z, self.rows].astype(F32)
         for k in (1, 2, 3):
-            acc = acc + self.ring[lax.rem(self.z + k, 4)].astype(F32)
+            acc = acc + self.ring[lax.rem(self.z + k, 4), self.rows].astype(F32)
         return acc
 
 
 class TensorGather:
-    def __init__(self, copies, buf, z, c):
-        self.c, self.buf, self.z, self.core = copies, buf, z, c
+    def __init__(self, copies, buf, z, c, lo=0, count=256):
+        self.c, self.buf, self.z, self.core, self.rows = copies, buf, z, c, pl.ds(lo, count)
 
     def along(self):
-        self.s = []
+        self.s = self.c.group()
         for k in (2, 1, 3):
-            mine = self.buf.at[self.core, self.z]
-            to = lax.rem(self.z + k, 4)
-            self.s.append(self.c.start(self.c.tags(1)[0], mine, mine, {"tensor_0": to}))
+            mine = self.buf.at[self.core, self.z, self.rows]
+            self.c.start(self.s, mine, mine, {"tensor_0": lax.rem(self.z + k, 4)})
 
     def across(self):
-        for copy in self.s:
-            copy.wait_recv()
+        self.c.arrived(self.s, self.buf.at[self.core, pl.ds(0, 3), self.rows], {"tensor_0": lax.rem(self.z + 1, 4)})
+        mine = self.buf.at[self.core, pl.ds(0, 4), self.rows]
+        self.x = self.c.group()
+        self.c.start(self.x, mine, mine, {"tensor_1": 1 - self.core})
+
+    def complete(self):
+        other = 1 - self.core
+        self.c.arrived(self.x, self.buf.at[other, pl.ds(0, 4), self.rows], {"tensor_1": other})
+
+
+class RingGather(TensorGather):
+    def along(self):
+        mine = self.buf.at[self.core, self.z]
+        self.o = self.c.group()
+        for k in (1, 3):
+            self.c.start(self.o, mine, mine, {"tensor_0": lax.rem(self.z + k, 4)})
+
+    def forward(self):
+        half = self.buf.shape[2] // 2
+        self.c.arrived(self.o, self.buf.at[self.core, pl.ds(0, 2)], {"tensor_0": lax.rem(self.z + 1, 4)})
+        self.f = self.c.group()
+        for k, lo in ((1, 0), (3, half)):
+            piece = self.buf.at[self.core, lax.rem(self.z + 4 - k, 4), pl.ds(lo, half)]
+            self.c.start(self.f, piece, piece, {"tensor_0": lax.rem(self.z + k, 4)})
+
+    def across(self):
+        far = self.buf.at[self.core, lax.rem(self.z + 2, 4)]
+        self.c.arrived(self.f, far, {"tensor_0": lax.rem(self.z + 1, 4)})
         mine = self.buf.at[self.core]
-        self.x = self.c.start(self.c.tags(1)[0], mine, mine, {"tensor_1": 1 - self.core})
+        self.x = self.c.group()
+        self.c.start(self.x, mine, mine, {"tensor_1": 1 - self.core})
 
     def complete(self):
-        self.x.wait_recv()
+        other = 1 - self.core
+        self.c.arrived(self.x, self.buf.at[other], {"tensor_1": other})
 
 
 class ScatterSum:
     def __init__(self, copies, buf, base, rows, got, y, x):
         self.c, self.buf, self.base, self.rows, self.got, self.y, self.x = copies, buf, base, rows, got, y, x
+        self.near = {"dp_0": lax.rem(y + 1, 4)}
 
     def axes(self, half):
         if half == 0:
@@ -245,37 +273,34 @@
 
     def one(self):
         r1 = self.got[0]
-        self.s1 = []
+        self.s1 = self.c.group()
         for half in (0, 1):
             b, pb, _, _ = self.axes(half)
             far = lax.rem(pb + 2, 4)
             for way, at, k in ((0, 0, 1), (1, 2, 3)):
                 src = self.slab(half, far, pl.ds(at, 2))
-                self.s1.append(
-                    self.c.start(self.c.tags(1)[0], src, r1.at[half, way], {b: lax.rem(pb + k, 4)})
-                )
+                self.c.start(self.s1, src, r1.at[half, way], {b: lax.rem(pb + k, 4)})
 
     def two(self):
         r1, r2 = self.got[0], self.got[1]
-        self.s2 = []
+        self.c.arrived(self.s1, r1, self.near)
+        self.s2 = self.c.group()
         for half in (0, 1):
             b, pb, _, _ = self.axes(half)
             for way, at, k in ((0, 0, 1), (1, 2, 3)):
                 to = lax.rem(pb + k, 4)
-                self.s1[2 * half + way].wait_recv()
                 for i in (0, 1):
                     mine = self.slab(half, to, at + i)
                     mine[...] = (mine[...].astype(F32) + r1[half, way, i].astype(F32)).astype(BF)
                 src = self.slab(half, to, pl.ds(0, 4))
-                self.s2.append(self.c.start(self.c.tags(1)[0], src, r2.at[half, way], {b: to}))
+                self.c.start(self.s2, src, r2.at[half, way], {b: to})
 
     def three(self):
         r2, r3 = self.got[1], self.got[2]
-        self.s3 = []
+        self.c.arrived(self.s2, r2, self.near)
+        self.s3 = self.c.group()
         for half in (0, 1):
             _, pb, a, pa = self.axes(half)
-            self.s2[2 * half].wait_recv()
-            self.s2[2 * half + 1].wait_recv()
 
             def add(i, carry):
                 k = lax.rem(pa + 2 + i, 4)
@@ -288,47 +313,28 @@
             far = lax.rem(pa + 2, 4)
             for way, lo, k in ((0, 0, 1), (1, self.rows // 2, 3)):
                 src = self.slab(half, pb, far, lo, lo + self.rows // 2)
-                self.s3.append(
-                    self.c.start(self.c.tags(1)[0], src, r3.at[half, way], {a: lax.rem(pa + k, 4)})
-                )
+                self.c.start(self.s3, src, r3.at[half, way], {a: lax.rem(pa + k, 4)})
             lax.fori_loop(1, 4, add, 0)
 
     def four(self):
         r3, r4 = self.got[2], self.got[3]
-        self.s4 = []
+        self.c.arrived(self.s3, r3, self.near)
+        self.s4 = self.c.group()
         for half in (0, 1):
             _, pb, a, pa = self.axes(half)
             for way, lo, k in ((0, 0, 1), (1, self.rows // 2, 3)):
                 to = lax.rem(pa + k, 4)
-                self.s3[2 * half + way].wait_recv()
                 mine = self.slab(half, pb, to, lo, lo + self.rows // 2)
                 mine[...] = (mine[...].astype(F32) + r3[half, way].astype(F32)).astype(BF)
-                src = self.slab(half, pb, to)
-                self.s4.append(self.c.start(self.c.tags(1)[0], src, r4.at[half, way], {a: to}))
+                self.c.start(self.s4, self.slab(half, pb, to), r4.at[half, way], {a: to})
 
     def five(self, half):
         r4 = self.got[3]
+        if half == 0:
+            self.c.arrived(self.s4, r4, self.near)
         _, pb, _, pa = self.axes(half)
-        self.s4[2 * half].wait_recv()
-        self.s4[2 * half + 1].wait_recv()
         mine = self.slab(half, pb, pa)
         return mine[...].astype(F32) + r4[half, 0].astype(F32) + r4[half, 1].astype(F32)
-
-
-class RingGather(TensorGather):
-    def along(self):
-        mine = self.buf.at[self.core, self.z]
-        self.o = [
-            self.c.start(self.c.tags(1)[0], mine, mine, {"tensor_0": lax.rem(self.z + k, 4)}) for k in (1, 3)
-        ]
-
-    def forward(self):
-        half = self.buf.shape[2] // 2
-        self.s = []
-        for copy, k, lo in zip(self.o, (1, 3), (0, half)):
-            copy.wait_recv()
-            piece = self.buf.at[self.core, lax.rem(self.z + 4 - k, 4), pl.ds(lo, half)]
-            self.s.append(self.c.start(self.c.tags(1)[0], piece, piece, {"tensor_0": lax.rem(self.z + k, 4)}))
 
 
 def blocks(ref, *lead, rows=slice(None)):
@@ -482,8 +488,15 @@
         sgather[l].across()
         sgather[l].complete()
 
-    gsum = [TensorSum(copies, gpart.at[l], gpair.at[l], gboth.at[l], gring.at[l], z, c) for l in (0, 1)]
-    ggather = [TensorGather(copies, gnew.at[l], z, c) for l in (0, 1)]
+    gsum = [
+        [
+            TensorSum(copies, gpart.at[l], gpair.at[l], gboth.at[l], gring.at[l], z, c, lo, 128)
+            for lo in (0, 128)
+        ]
+        for l in (0, 1)
+    ]
+    ggather = [[TensorGather(copies, gnew.at[l], z, c, lo, 128) for lo in (0, 128)] for l in (0, 1)]
+    halves = (pl.ds(0, 128), pl.ds(128, 128))
     scatter = {}
     for i, (key, k, first, rows) in enumerate(CHUNKS):
         scatter[key] = ScatterSum(copies, wg.at[k], first, rows, sums[4 * i:4 * i + 4], y, x)
@@ -595,13 +608,11 @@
             (stat_t, t, [(0, {"tensor_0": o // 2, "tensor_1": lax.rem(o, 2)}) for o in others]),
         )
         for i, (got, me, targets) in enumerate(steps):
-            sent = [
-                copies.start(copies.tags(1)[0], stat.at[i], got.at[me], where) for _, where in targets
-            ]
-            acc = stat[i]
-            got[me] = acc
-            for copy in sent:
-                copy.wait_recv()
+            group = copies.group()
+            for _, where in targets:
+                copies.start(group, stat.at[i], got.at[me], where)
+            got[me] = stat[i]
+            copies.arrived(group, got.at[pl.ds(0, len(targets))], targets[0][1])
             total = got[0]
             for k in range(1, got.shape[0]):
                 total = total + got[k]
@@ -659,48 +670,58 @@
     teacher_down(1, 0)
     teacher_down(1, 1)
     top_part()
-    gsum[1].across()
+    for half in (0, 1):
+        gsum[1][half].across()
     tsum[1].across()
-    gsum[1].along()
+    for half in (0, 1):
+        gsum[1][half].along()
     gu[0].sent()
     gu[1].sent()
-    late = gsum[1].total()
-    gwide[...] = base[1] - jnp.where(lmap[1] == 1, late, 0.0)
-    gnew[1, c, z] = gwide[...].astype(BF)
-    ggather[1].along()
+    for half, rows in enumerate(halves):
+        late = gsum[1][half].total()
+        g = base[1, rows] - jnp.where(lmap[1] == 1, late, 0.0)
+        gnew[1, c, z, rows] = g.astype(BF)
+        ggather[1][half].along()
+        gwide[rows] = g + base[0, rows] - jnp.where(lmap[0] == 1, late, 0.0)
     tsum[1].along()
-    gwide[...] = gwide[...] + base[0] - jnp.where(lmap[0] == 1, late, 0.0)
-    ggather[1].across()
-    ggather[1].complete()
-    sn[1] = blocks(gnew, 1)
+    for half in (0, 1):
+        ggather[1][half].across()
+    for half, rows in enumerate(halves):
+        ggather[1][half].complete()
+        sn[1, rows] = blocks(gnew, 1, rows=rows)
     down_grad(1)
     units_back(1)
     norm_part()
-    gsum[0].across()
-    unit_grads(1)
-    gsum[0].along()
+    for half in (0, 1):
+        gsum[0][half].across()
+    weight_grad("g1", snt.at[1], ga.at[1])
+    for half in (0, 1):
+        gsum[0][half].along()
+    weight_grad("u1", snt.at[1], gb.at[1])
     scatter["d1"].two()
-    gwide[...] = gwide[...] + gsum[0].total()
-    gnew[0, c, z] = gwide[...].astype(BF)
-    ggather[0].along()
+    for half, rows in enumerate(halves):
+        gnew[0, c, z, rows] = (gwide[rows] + gsum[0][half].total()).astype(BF)
+        ggather[0][half].along()
     scatter["g1"].two()
     teacher_result(1)
     e1 = error(1)
     e0 = error(0)
-    shared = []
+    shared = copies.group()
     for o in others:
         rows = pl.ds(pl.multiple_of(o * 32, 32), 32)
         where = {"tensor_0": o // 2, "tensor_1": lax.rem(o, 2)}
-        shared.append(copies.start(copies.tags(1)[0], hn.at[1, c, z, rows], rows_in.at[t], where))
+        copies.start(shared, hn.at[1, c, z, rows], rows_in.at[t], where)
     rows_in[t] = hn[1, c, z, pl.ds(pl.multiple_of(t * 32, 32), 32), :]
     proj_grad()
     scatter["p"].one()
     scatter["u1"].two()
-    ggather[0].across()
+    for half in (0, 1):
+        ggather[0][half].across()
     scatter["d1"].three()
     scatter["p"].two()
-    ggather[0].complete()
-    sn[0] = blocks(gnew, 0)
+    for half, rows in enumerate(halves):
+        ggather[0][half].complete()
+        sn[0, rows] = blocks(gnew, 0, rows=rows)
     down_grad(0)
     units_back(0)
     unit_grads(0)
@@ -720,8 +741,7 @@
     grad_end("g1")
     scatter["g0"].three()
     grad_end("u1")
-    for copy in shared:
-        copy.wait_recv()
+    copies.arrived(shared, rows_in.at[pl.ds(0, 7)], peers[-1])
     for i in range(8):
         states_out[1, :, i * 256:(i + 1) * 256] = rows_in[i]
     scatter["u0"].three()
@@ -826,8 +846,8 @@
             VMEM((3, 8, 128), F32),
             VMEM((16, 8, 128), F32),
             VMEM((8, 8, 128), F32),
-            pltpu.SemaphoreType.DMA((N_COPY,)),
-            pltpu.SemaphoreType.DMA((N_COPY,)),
+            pltpu.SemaphoreType.DMA((N_SEND,)),
+            pltpu.SemaphoreType.DMA((N_RECV,)),
             pltpu.SemaphoreType.DMA((N_LOCAL,)),
         ],
         compiler_params=pltpu.CompilerParams(

time: 185 us -> 180 us (0.973)
  Pallas kernels: 181 us -> 176 us
    pallas_call x1, Pallas kernels: 178 us -> 173 us  [run(): pl.pallas_call(step_kernel, out_shape=(shape((2, 32, 2048), BF), shape((2...]
where the time goes in v5:
time: 180 us
  Pallas kernels  176 us (98%)
  local copies, waits for them, and re-layouts  3.79 us (2%)
    pallas_call x1, Pallas kernels, run(): pl.pallas_call(step_kernel, out_shape=(shape((2, 32, 2048), BF), shape((2...  173 us

profile of v5, /device:TPU:1, one launch (start us, length us, event | category | flops | bytes accessed | tf_op | source)
XLA Modules:
  0.0 180.1 jit_solution(15279511591346437050)
XLA Ops:
  0.6 1.8 copy.21.dn_in
  2.4 2.0 %copy_bitcast_fusion = (bf16[2,684,128]{2,1,0:T(8,128)(2,1)}, bf16[2,684,128]{2,1,0:T(8,128)(2,1)}) fusion(bf16[2,128,684]{1,0,2:T(2,128)(2,1)} %param.15, bf16[2,128,684]{1,0,2:T(2,128)(2,1)} %param.14), kind=kLoop, calls=%fused_computation | loop fusion | bytes 1400832 | tf_op jit(solution)/shard_map/transpose | solution.py:866
  4.4 173.3 %step.1 = (bf16[2,32,2048]{2,1,0:T(8,128)(2,1)}, f32[2,64,512]{2,1,0:T(8,128)}, f32[2,64,512]{2,1,0:T(8,128)}, f32[2,64,512]{2,1,0:T(8,128)}, f32[64,256]{1,0:T(8,128)}, /*index=5*/f32[8,128]{1,0:T(8,128)}) custom-call(s32[2]{0:T(128)} %lmap.1, bf16[256,2048]{1,0:T(8,128)(2,1)} %tin.1, f32[2,2048]{1,0:T(2,128)} %tgain.1, bf16[256,1024]{1,0:T(8,128)(2,1)} %sin.1, ...), custom_call_target="tpu_custom_call" | custom-call | tf_op jit(solution)/shard_map/step/pallas_call | solution.py:789
  177.7 2.2 %finish.1 = (bf16[2,32,2048]{2,1,0:T(8,128)(2,1)}, f32[2,64,512]{2,1,0:T(8,128)}, f32[2,64,512]{2,1,0:T(8,128)}, f32[2,64,512]{2,1,0:T(8,128)}, f32[64,256]{1,0:T(8,128)}, /*index=5*/f32[2]{0:T(128)}, f32[4]{0:T(128)}) custom-call(f32[8,128]{1,0:T(8,128)} %get-tuple-element.20.stats, bf16[2,32,2048]{2,1,0:T(8,128)(2,1)} %get-tuple-element.21.refs_0_, ...), custom_call_target="tpu_custom_call" | custom-call | tf_op jit(solution)/shard_map/finish/pallas_call | solution.py:775

commit v6 on v5

--- a/solution.py
+++ b/solution.py
@@ -23,7 +23,7 @@
 F32 = jnp.float32
 N_SEND = 64
 N_RECV = 110
-N_LOCAL = 11
+N_LOCAL = 24
 GU_HALVES = ((0, 352, 688), (688, 1040, 1376))
 CHUNKS = (
     ("d1", 0, 0, 128),
@@ -258,8 +258,9 @@
 
 
 class ScatterSum:
-    def __init__(self, copies, buf, base, rows, got, y, x):
+    def __init__(self, copies, buf, base, rows, got, y, x, direct=False):
         self.c, self.buf, self.base, self.rows, self.got, self.y, self.x = copies, buf, base, rows, got, y, x
+        self.direct = direct
         self.near = {"dp_0": lax.rem(y + 1, 4)}
 
     def axes(self, half):
@@ -309,6 +310,13 @@
                 mine[...] = (mine[...].astype(F32) + both).astype(BF)
                 return carry
 
+            if self.direct:
+                for i, k in ((0, 2), (3, 1), (1, 3)):
+                    add(i, 0)
+                    to = lax.rem(pa + k, 4)
+                    self.c.start(self.s3, self.slab(half, pb, to), self.got[4].at[half, k - 1], {a: to})
+                add(2, 0)
+                continue
             add(0, 0)
             far = lax.rem(pa + 2, 4)
             for way, lo, k in ((0, 0, 1), (1, self.rows // 2, 3)):
@@ -317,6 +325,8 @@
             lax.fori_loop(1, 4, add, 0)
 
     def four(self):
+        if self.direct:
+            return
         r3, r4 = self.got[2], self.got[3]
         self.c.arrived(self.s3, r3, self.near)
         self.s4 = self.c.group()
@@ -330,6 +340,14 @@
 
     def five(self, half):
         r4 = self.got[3]
+        if self.direct:
+            if half == 0:
+                self.c.arrived(self.s3, self.got[4], self.near)
+            _, pb, _, pa = self.axes(half)
+            total = self.slab(half, pb, pa)[...].astype(F32)
+            for k in range(3):
+                total = total + self.got[4][half, k].astype(F32)
+            return total
         if half == 0:
             self.c.arrived(self.s4, r4, self.near)
         _, pb, _, pa = self.axes(half)
@@ -342,8 +360,9 @@
 
 
 def step_kernel(
-    lmap, tin, tgain, sin, sgain, gate_in, up_in, dn_in, sg_in, su_in, sd_in, proj_in,
-    states_out, gate_out, up_out, down_out, proj_out, mean_out,
+    lmap_in, tin_in, tgain_in, sin_in, sgain_in, gate_in, up_in, dn_in, sg_in, su_in, sd_in, proj_in,
+    states_to, gate_to, up_to, down_to, proj_to, mean_to,
+    lmap, tin, tgain, sin, sgain, states_out, gate_out, up_out, down_out, proj_out, mean_out,
     wg, wd, sg, su, sd, pf, xs, tn, acts, hid, sn, snt, a_out, b_out, u_out,
     spart, spair, sboth, sring, tpart, tpair, tboth, tring, hn, rows_in,
     pred, delta, gpart, gpair, gboth, gring, gnew, gwide, gyt, ga, gb, base, *rest,
@@ -383,14 +402,17 @@
     load(su_in, su)
     load(sd_in, sd)
     load(proj_in, pf.at[c, z])
+    for src, dst in ((lmap_in, lmap), (tin_in, tin), (tgain_in, tgain), (sin_in, sin), (sgain_in, sgain)):
+        load(src, dst)
     gu = [Gather(copies, wg.at[l], GU_HALVES, y, x) for l in (0, 1)]
     dn = [Gather(copies, wd.at[l], DN_HALVES, y, x) for l in (0, 1)]
     pl.semaphore_wait(barrier, len(peers))
-    loads[0].wait()
-    loads[1].wait()
-    gu[0].first()
-    loads[2].wait()
-    dn[0].first()
+    for l in (0, 1):
+        for copy in loads[3 * l:3 * l + 2]:
+            copy.wait()
+        gu[l].first()
+        loads[3 * l + 2].wait()
+        dn[l].first()
 
     def teacher_norm(k):
         def body(r):
@@ -499,7 +521,7 @@
     halves = (pl.ds(0, 128), pl.ds(128, 128))
     scatter = {}
     for i, (key, k, first, rows) in enumerate(CHUNKS):
-        scatter[key] = ScatterSum(copies, wg.at[k], first, rows, sums[4 * i:4 * i + 4], y, x)
+        scatter[key] = ScatterSum(copies, wg.at[k], first, rows, sums[5 * i:5 * i + 5], y, x, key in ("g0", "u0"))
 
     def error(l):
         target = jnp.where(lmap[l] == 0, hn[0, c, z].astype(F32), hn[1, c, z].astype(F32))
@@ -621,23 +643,18 @@
 
     loads[9].wait()
     pgather.along()
+    for copy in loads[10:]:
+        copy.wait()
     teacher_norm(0)
-    gu[0].first_forward()
-    dn[0].first_forward()
+    for g in (gu[0], dn[0], gu[1], dn[1]):
+        g.first_forward()
     gu[0].second()
-    loads[3].wait()
-    loads[4].wait()
-    gu[1].first()
-    loads[5].wait()
-    dn[1].first()
     dn[0].second()
     student(0)
     pgather.forward()
     student_end(0)
     pgather.across()
     gu[0].second_forward()
-    gu[1].first_forward()
-    dn[1].first_forward()
     student(1)
     student_end(1)
     pgather.complete()
@@ -689,11 +706,11 @@
     for half, rows in enumerate(halves):
         ggather[1][half].complete()
         sn[1, rows] = blocks(gnew, 1, rows=rows)
-    down_grad(1)
     units_back(1)
     norm_part()
     for half in (0, 1):
         gsum[0][half].across()
+    down_grad(1)
     weight_grad("g1", snt.at[1], ga.at[1])
     for half in (0, 1):
         gsum[0][half].along()
@@ -744,17 +761,26 @@
     copies.arrived(shared, rows_in.at[pl.ds(0, 7)], peers[-1])
     for i in range(8):
         states_out[1, :, i * 256:(i + 1) * 256] = rows_in[i]
+    first_store = len(loads)
+    load(states_out, states_to)
+    load(proj_out, proj_to)
     scatter["u0"].three()
     scatter["d0"].four()
     scatter["g0"].four()
     scatter["u0"].four()
     grad_end("d0")
+    load(down_out, down_to)
     grad_end("g0")
+    load(gate_out, gate_to)
     grad_end("u0")
+    load(up_out, up_to)
     total = totals([e0, e1] + [found[k] for k in "gudp"])
     mean_out[0:2, :] = total[0:2] / float(4096 * DT)
     mean_out[2:5, :] = jnp.sqrt(total[2:5] / float(S_LAYERS * DS * FS))
     mean_out[5:8, :] = jnp.sqrt(total[5:8] / float(DS * DT))
+    load(mean_out, mean_to)
+    for copy in loads[first_store:]:
+        copy.wait()
     copies.finish()
 
 
@@ -782,9 +808,8 @@
     )(stats, *arrays)
 
 
-def run(lmap, tin, tgain, sin, sgain, gate, up, dn, sg, su, sd, proj):
+def run(*arrays):
     shape = jax.ShapeDtypeStruct
-    here = pl.BlockSpec(memory_space=VMEM)
     away = pl.BlockSpec(memory_space=pl.ANY)
     return pl.pallas_call(
         step_kernel,
@@ -796,9 +821,20 @@
             shape((64, 256), F32),
             shape((8, 128), F32),
         ),
-        in_specs=[pl.BlockSpec(memory_space=pltpu.SMEM)] + [here] * 4 + [away] * 7,
-        out_specs=(here,) * 6,
+        in_specs=[away] * len(arrays),
+        out_specs=(away,) * 6,
         scratch_shapes=[
+            pltpu.SMEM((2,), jnp.int32),
+            VMEM((256, 2048), BF),
+            VMEM((2, 2048), F32),
+            VMEM((256, 1024), BF),
+            VMEM((2, 1024), F32),
+            VMEM((2, 32, 2048), BF),
+            VMEM((2, 64, 512), F32),
+            VMEM((2, 64, 512), F32),
+            VMEM((2, 64, 512), F32),
+            VMEM((64, 256), F32),
+            VMEM((8, 128), F32),
             VMEM((2, 4, 4, 1376, 128), BF),
             VMEM((2, 4, 4, 688, 128), BF),
             VMEM((2, 1024, 512), BF),
@@ -840,7 +876,7 @@
         + [
             VMEM(s, BF)
             for _, _, _, r in CHUNKS
-            for s in ((2, 2, 2, r, 128), (2, 2, 4, r, 128), (2, 2, r // 2, 128), (2, 2, r, 128))
+            for s in ((2, 2, 2, r, 128), (2, 2, 4, r, 128), (2, 2, r // 2, 128), (2, 2, r, 128), (2, 3, r, 128))
         ]
         + [
             VMEM((3, 8, 128), F32),
@@ -854,7 +890,7 @@
             collective_id=0, has_side_effects=True, vmem_limit_bytes=67043328
         ),
         name="step",
-    )(lmap, tin, tgain, sin, sgain, gate, up, dn, sg, su, sd, proj)
+    )(*arrays)
 
 
 def per_device(

time: 180 us -> 178 us (0.989)
  Pallas kernels: 176 us -> 173 us
    pallas_call x1, Pallas kernels: 173 us -> 171 us  [run(): pl.pallas_call(step_kernel, out_shape=(shape((2, 32, 2048), BF), shape((2...]
where the time goes in v6:
time: 178 us; the launch traced here: 177 us
  Pallas kernels  173 us (97%)
  local copies, waits for them, and re-layouts  3.79 us (2%)
    pallas_call x1, Pallas kernels, run(): pl.pallas_call(step_kernel, out_shape=(shape((2, 32, 2048), BF), shape((2...  171 us

profile of v6, /device:TPU:1, one launch (start us, length us, event | category | flops | bytes accessed | tf_op | source)
XLA Modules:
  0.0 177.5 jit_solution(13705913056025840778)
XLA Ops:
  0.6 1.8 copy.21.dn_in
  2.4 2.0 %copy_bitcast_fusion = (bf16[2,684,128]{2,1,0:T(8,128)(2,1)}, bf16[2,684,128]{2,1,0:T(8,128)(2,1)}) fusion(bf16[2,128,684]{1,0,2:T(2,128)(2,1)} %param.15, bf16[2,128,684]{1,0,2:T(2,128)(2,1)} %param.14), kind=kLoop, calls=%fused_computation | loop fusion | bytes 1400832 | tf_op jit(solution)/shard_map/transpose | solution.py:902
  4.4 170.7 %step.1 = (bf16[2,32,2048]{2,1,0:T(8,128)(2,1)}, f32[2,64,512]{2,1,0:T(8,128)}, f32[2,64,512]{2,1,0:T(8,128)}, f32[2,64,512]{2,1,0:T(8,128)}, f32[64,256]{1,0:T(8,128)}, /*index=5*/f32[8,128]{1,0:T(8,128)}) custom-call(s32[2]{0:T(128)} %lmap_in.1, bf16[256,2048]{1,0:T(8,128)(2,1)} %tin_in.1, f32[2,2048]{1,0:T(2,128)} %tgain_in.1, bf16[256,1024]{1,0:T(8,128)(2,1)} %sin_in.1, ...), custom_call_target="tpu_custom_call" | custom-call | tf_op jit(solution)/shard_map/step/pallas_call | solution.py:814
  175.1 2.2 %finish.1 = (bf16[2,32,2048]{2,1,0:T(8,128)(2,1)}, f32[2,64,512]{2,1,0:T(8,128)}, f32[2,64,512]{2,1,0:T(8,128)}, f32[2,64,512]{2,1,0:T(8,128)}, f32[64,256]{1,0:T(8,128)}, /*index=5*/f32[2]{0:T(128)}, f32[4]{0:T(128)}) custom-call(f32[8,128]{1,0:T(8,128)} %get-tuple-element.20.stats, bf16[2,32,2048]{2,1,0:T(8,128)(2,1)} %get-tuple-element.21.refs_0_, ...), custom_call_target="tpu_custom_call" | custom-call | tf_op jit(solution)/shard_map/finish/pallas_call | solution.py:801

commit v7 on v6

--- a/solution.py
+++ b/solution.py
@@ -21,9 +21,9 @@
 MESH = pl.DeviceIdType.MESH
 BF = jnp.bfloat16
 F32 = jnp.float32
-N_SEND = 64
-N_RECV = 110
-N_LOCAL = 24
+N_SEND = 40
+N_RECV = 100
+N_LOCAL = 21
 GU_HALVES = ((0, 352, 688), (688, 1040, 1376))
 CHUNKS = (
     ("d1", 0, 0, 128),

time: 178 us -> 177 us (level)
  no operation moved by 1% of the time
where the time goes in v7:
time: 177 us
  Pallas kernels  173 us (98%)
  local copies, waits for them, and re-layouts  3.79 us (2%)
    pallas_call x1, Pallas kernels, run(): pl.pallas_call(step_kernel, out_shape=(shape((2, 32, 2048), BF), shape((2...  170 us

profile of v7, /device:TPU:1, one launch (start us, length us, event | category | flops | bytes accessed | tf_op | source)
XLA Modules:
  0.0 177.2 jit_solution(7966449775349242986)
XLA Ops:
  0.6 1.8 copy.21.dn_in
  2.4 2.0 %copy_bitcast_fusion = (bf16[2,684,128]{2,1,0:T(8,128)(2,1)}, bf16[2,684,128]{2,1,0:T(8,128)(2,1)}) fusion(bf16[2,128,684]{1,0,2:T(2,128)(2,1)} %param.15, bf16[2,128,684]{1,0,2:T(2,128)(2,1)} %param.14), kind=kLoop, calls=%fused_computation | loop fusion | bytes 1400832 | tf_op jit(solution)/shard_map/transpose | solution.py:902
  4.4 170.4 %step.1 = (bf16[2,32,2048]{2,1,0:T(8,128)(2,1)}, f32[2,64,512]{2,1,0:T(8,128)}, f32[2,64,512]{2,1,0:T(8,128)}, f32[2,64,512]{2,1,0:T(8,128)}, f32[64,256]{1,0:T(8,128)}, /*index=5*/f32[8,128]{1,0:T(8,128)}) custom-call(s32[2]{0:T(128)} %lmap_in.1, bf16[256,2048]{1,0:T(8,128)(2,1)} %tin_in.1, f32[2,2048]{1,0:T(2,128)} %tgain_in.1, bf16[256,1024]{1,0:T(8,128)(2,1)} %sin_in.1, ...), custom_call_target="tpu_custom_call" | custom-call | tf_op jit(solution)/shard_map/step/pallas_call | solution.py:814
  174.9 2.2 %finish.1 = (bf16[2,32,2048]{2,1,0:T(8,128)(2,1)}, f32[2,64,512]{2,1,0:T(8,128)}, f32[2,64,512]{2,1,0:T(8,128)}, f32[2,64,512]{2,1,0:T(8,128)}, f32[64,256]{1,0:T(8,128)}, /*index=5*/f32[2]{0:T(128)}, f32[4]{0:T(128)}) custom-call(f32[8,128]{1,0:T(8,128)} %get-tuple-element.20.stats, bf16[2,32,2048]{2,1,0:T(8,128)(2,1)} %get-tuple-element.21.refs_0_, ...), custom_call_target="tpu_custom_call" | custom-call | tf_op jit(solution)/shard_map/finish/pallas_call | solution.py:801
